TPU v7x, 8 devices: a whole 2x2x1 slice. The times are simulated.
8 devices in a mesh: dp: 1 (over z), tp: 8 (over y, x, core).
Axes of the slice: x: 2, y: 2, z: 1, core: 2. Of those that a mesh axis runs over, the one named last changes fastest.
Arguments:
- tokens_in: bfloat16 [32, 256, 1280], P('dp')
- ln_scale: bfloat16 [2, 1280], replicated
- w_query: bfloat16 [2, 1280, 1280], P(None, None, 'tp')
- w_key: bfloat16 [2, 1280, 1280], P(None, None, 'tp')
- w_value: bfloat16 [2, 1280, 1280], P(None, None, 'tp')
- q_scale: bfloat16 [2, 80], replicated
- k_scale: bfloat16 [2, 80], replicated
- w_out: bfloat16 [2, 1280, 1280], P(None, 'tp')
- b_out: bfloat16 [2, 1280], replicated
- w_up: bfloat16 [2, 1280, 5120], P(None, None, 'tp')
- b_up: bfloat16 [2, 5120], P(None, 'tp')
- w_down: bfloat16 [2, 5120, 1280], P(None, 'tp')
- b_down: bfloat16 [2, 1280], replicated
Outputs:
- output: bfloat16 [32, 256, 1280], P('dp')
All inputs are finite; a program needn't handle non-finite values.
Results may differ from a plain program's by a relative error of at most 0.0129673.
Values are sent between devices in bfloat16 or wider.
A program may use at most 1 GiB of HBM per device.

v0:
```python
import jax
import jax.numpy as jnp
from jax import lax
from jax.sharding import PartitionSpec as P

LN_EPS = 1e-6


def layer_norm(values, scale_vec):
    mean_val = jnp.mean(values, axis=-1, keepdims=True)
    centered = values - mean_val
    variance = jnp.mean(centered * centered, axis=-1, keepdims=True)
    return centered * lax.rsqrt(variance + LN_EPS) * scale_vec.astype(jnp.float32)


def local_branches(normed, n_images, seq_len, w_query, w_key, w_value, q_scale, k_scale, w_out, w_up, b_up, w_down):
    head_dim = q_scale.shape[0]
    local_heads = w_query.shape[1] // head_dim

    def project(weight):
        projected = jnp.dot(normed, weight, preferred_element_type=jnp.float32)
        return projected.reshape(n_images, seq_len, local_heads, head_dim)

    queries = layer_norm(project(w_query), q_scale).astype(jnp.bfloat16)
    keys_all = layer_norm(project(w_key), k_scale).astype(jnp.bfloat16)
    values_all = project(w_value).astype(jnp.bfloat16)
    scores = jnp.einsum("bqhd,bkhd->bhqk", queries, keys_all, preferred_element_type=jnp.float32) * head_dim ** -0.5
    attn_prob = jax.nn.softmax(scores, axis=-1).astype(jnp.bfloat16)
    mixed_val = jnp.einsum("bhqk,bkhd->bqhd", attn_prob, values_all, preferred_element_type=jnp.float32)
    mixed_val = mixed_val.astype(jnp.bfloat16).reshape(n_images * seq_len, local_heads * head_dim)
    attn_part = jnp.dot(mixed_val, w_out, preferred_element_type=jnp.float32)
    pre_act = jnp.dot(normed, w_up, preferred_element_type=jnp.float32) + b_up.astype(jnp.float32)
    activated = jax.nn.gelu(pre_act, approximate=True).astype(jnp.bfloat16)
    return attn_part + jnp.dot(activated, w_down, preferred_element_type=jnp.float32)


def solution(mesh):
    col_spec = P(None, None, "tp")
    row_spec = P(None, "tp", None)
    in_specs = (P("dp", None, None), P(), col_spec, col_spec, col_spec, P(), P(), row_spec, P(), col_spec, P(None, "tp"), row_spec, P())

    def per_device(tokens_in, ln_scale, w_query, w_key, w_value, q_scale, k_scale, w_out, b_out, w_up, b_up, w_down, b_down):
        n_images, seq_len, model_dim = tokens_in.shape
        n_tokens = n_images * seq_len
        current = tokens_in
        for layer_idx in range(w_query.shape[0]):
            residual = current.reshape(n_tokens, model_dim).astype(jnp.float32)
            normed = layer_norm(residual, ln_scale[layer_idx]).astype(jnp.bfloat16)
            part_sum = local_branches(normed, n_images, seq_len, w_query[layer_idx], w_key[layer_idx], w_value[layer_idx], q_scale[layer_idx], k_scale[layer_idx], w_out[layer_idx], w_up[layer_idx], b_up[layer_idx], w_down[layer_idx])
            reduced = lax.psum(part_sum.astype(jnp.bfloat16), "tp")
            summed = residual + b_out[layer_idx].astype(jnp.float32) + b_down[layer_idx].astype(jnp.float32) + reduced.astype(jnp.float32)
            current = summed.astype(jnp.bfloat16).reshape(n_images, seq_len, model_dim)
        return current

    return jax.shard_map(per_device, mesh=mesh, in_specs=in_specs, out_specs=P("dp", None, None), check_vma=False)
```

profile of v0, /device:TPU:0, one launch (start us, length us, event | category | flops | bytes accessed | tf_op | source)
XLA Modules:
  0.0 910.8 jit_solution(13538922858849531395)
XLA Ops:
  8.0 1.7 convert_reduce_fusion.2
  9.7 11.8 %convert_reduce_fusion.1 = f32[32,256]{1,0:T(8,128)S(1)} fusion(bf16[32,256,1280]{2,1,0:T(8,128)(2,1)} %param.13), kind=kLoop, calls=%fused_computation.21 | loop fusion | flops 20963328 | bytes 21004288 | tf_op jit(solution)/shard_map/reduce_sum | solution.py:10
  21.6 7.7 multiply_reduce_fusion
  32.0 7.6 multiply_convert_fusion
  39.5 10.0 %fusion.106 = (f32[32,256,2]{1,2,0:T(2,128)S(1)}, f32[32,256,2,80]{1,3,2,0:T(8,128)}) fusion(bf16[2,80,1280,1]{2,1,0,3:T(8,128)(2,1)} %bitcast.173, bf16[32,256,1280]{2,1,0:T(8,128)(2,1)S(1)} %multiply_convert_fusion), kind=kOutput, calls=%fused_computation.137 | convolution fusion | flops 3356737536 | bytes 26689536 | tf_op jit(solution)/shard_map/dot_general | solution.py:21
  49.6 8.7 fusion.105
  59.0 3.6 multiply_reduce_fusion.6
  62.6 3.6 multiply_reduce_fusion.5
  66.3 12.7 %fusion.47 = f32[32,2,256,256]{2,3,1,0:T(8,128)} fusion(f32[32,256,2,80]{1,3,2,0:T(8,128)} %get-tuple-element.28, f32[32,256,2,80]{1,3,2,0:T(8,128)} %get-tuple-element.26, f32[80]{0:T(128)S(1)} %get-tuple-element.24, f32[32,256,2]{1,2,0:T(2,128)S(1)} %get-tuple-element.37, f32[32,256,2]{1,2,0:T(2,128)S(1)} %broadcast_multiply_fusion.2, ...), kind=kOutput, calls=%fused_computation.68 | convolution fusion | flops 681574400 | bytes 27525760 | tf_op jit(solution)/shard_map/bqhd,bkhd->bhqk/dot_general | solution.py:27
  79.0 19.4 %fusion.107 = (f32[32,2,256]{2,1,0:T(2,128)S(1)}, f32[32,2,256,256]{2,3,1,0:T(8,128)}) fusion(f32[32,2,256,256]{2,3,1,0:T(8,128)} %fusion.47), kind=kOutput, calls=%fused_computation.138 | output fusion | flops 16777472 | bytes 33619968 | tf_op jit(solution)/shard_map/sub | solution.py:28
  98.5 16.0 %convert_bitcast_fusion.1 = bf16[32,256,2,80]{1,3,2,0:T(8,128)(2,1)S(1)} fusion(f32[32,2,256,256]{2,3,1,0:T(8,128)} %get-tuple-element.30, f32[32,2,256]{2,1,0:T(2,128)S(1)} %get-tuple-element.29, bf16[2,80,1280,1]{2,1,0,3:T(8,128)(2,1)S(1)} %bitcast.171, bf16[32,256,1280]{2,1,0:T(8,128)(2,1)} %copy-done.2), kind=kOutput, calls=%fused_computation.79 | convolution fusion | flops 4037541888 | bytes 40845312 | tf_op jit(solution)/shard_map/bhqk,bkhd->bqhd/dot_general | solution.py:29
  116.0 1.8 copy.24
  117.8 23.1 %fusion.20.clone.5 = bf16[8192,640]{1,0:T(8,128)(2,1)S(1)} fusion(bf16[8192,1280]{1,0:T(8,128)(2,1)} %bitcast.160, f32[640]{0:T(1024)S(1)} %get-tuple-element.12, bf16[2,1280,640]{2,1,0:T(8,128)(2,1)} %param.22), kind=kOutput, calls=%fused_computation.31.clone.clone.clone.2 | convolution fusion | flops 13474201600 | bytes 33098240 | tf_op jit(solution)/shard_map/dot_general | solution.py:32
  140.9 21.8 %fusion.46 = f32[8192,1280]{1,0:T(8,128)} fusion(bf16[2,640,1280]{2,1,0:T(8,128)(2,1)S(1)} %copy-done.22, bf16[8192,640]{1,0:T(8,128)(2,1)S(1)} %fusion.20.clone.5), kind=kOutput, calls=%fused_computation.67 | convolution fusion | flops 13421772800 | bytes 54067200 | tf_op jit(solution)/shard_map/dot_general | solution.py:34
  162.7 21.0 %add_convert_fusion.1 = bf16[8192,1280]{1,0:T(8,128)(2,1)} fusion(f32[8192,1280]{1,0:T(8,128)} %fusion.46, bf16[8192,160]{0,1:T(8,128)(2,1)S(1)} %bitcast.165, bf16[2,160,1280]{2,1,0:T(8,128)(2,1)S(1)} %copy-done.4), kind=kOutput, calls=%fused_computation.18 | convolution fusion | flops 3376414720 | bytes 65945600 | tf_op jit(solution)/shard_map/dot_general | solution.py:31
  185.0 253.0 %all-reduce.3.cloned.1.call-done = bf16[8192,1280]{1,0:T(8,128)(2,1)} async-done(((bf16[8192,1280]{1,0:T(8,128)(2,1)}), bf16[8192,1280]{1,0:T(8,128)(2,1)}) %all-reduce.3.cloned.1.call-update) | async-done | bytes 20971536 | tf_op jit(solution)/shard_map/psum | solution.py:50
  438.0 22.1 %convert_reduce_fusion = (f32[8192]{0:T(1024)S(1)}, bf16[8192,1280]{1,0:T(8,128)(2,1)}) fusion(bf16[8192,1280]{1,0:T(8,128)(2,1)} %all-reduce.3.cloned.1.call-done, f32[1280]{0:T(1024)S(1)} %get-tuple-element.8, f32[1280]{0:T(1024)S(1)} %get-tuple-element.41, bf16[32,256,1280]{2,1,0:T(8,128)(2,1)} %param.13), kind=kLoop, calls=%fused_computation.3 | loop fusion | flops 83877888 | bytes 62957568 | tf_op jit(solution)/shard_map/reduce_sum | solution.py:10
  460.1 17.4 %fusion.4 = f32[8192]{0:T(1024)S(1)} fusion(bf16[8192,1280]{1,0:T(8,128)(2,1)} %get-tuple-element.14, f32[8192]{0:T(1024)S(1)} %broadcast_multiply_fusion.4), kind=kLoop, calls=%fused_computation.7 | loop fusion | flops 41934848 | bytes 21037056 | tf_op jit(solution)/shard_map/reduce_sum | solution.py:12
  477.6 7.7 fusion.6
  485.3 8.7 fusion.109
  494.0 3.6 multiply_reduce_fusion.4
  497.7 8.9 fusion.108
  506.7 3.6 multiply_reduce_fusion.3
  510.4 12.8 %fusion.48 = f32[32,2,256,256]{2,3,1,0:T(8,128)} fusion(f32[32,256,2,80]{1,3,2,0:T(8,128)} %get-tuple-element.34, f32[32,256,2,80]{1,3,2,0:T(8,128)} %get-tuple-element.32, f32[80]{0:T(128)S(1)} %copy-done.18, f32[32,256,2]{1,2,0:T(2,128)S(1)} %add_rsqrt_fusion, f32[32,256,2]{1,2,0:T(2,128)S(1)} %broadcast_multiply_fusion, f32[80]{0:T(128)S(1)} %copy-done.19, ...), kind=kOutput, calls=%fused_computation.69 | convolution fusion | flops 681574400 | bytes 27525760 | tf_op jit(solution)/shard_map/bqhd,bkhd->bhqk/dot_general | solution.py:27
  523.2 19.3 %fusion.110 = (f32[32,2,256]{2,1,0:T(2,128)S(1)}, f32[32,2,256,256]{2,3,1,0:T(8,128)}) fusion(f32[32,2,256,256]{2,3,1,0:T(8,128)} %fusion.48), kind=kOutput, calls=%fused_computation.141 | output fusion | flops 16777472 | bytes 33619968 | tf_op jit(solution)/shard_map/sub | solution.py:28
  542.5 16.4 %convert_bitcast_fusion = bf16[32,256,2,80]{1,3,2,0:T(8,128)(2,1)S(1)} fusion(f32[32,2,256,256]{2,3,1,0:T(8,128)} %get-tuple-element.36, f32[32,2,256]{2,1,0:T(2,128)S(1)} %get-tuple-element.35, bf16[32,256,1280,1]{2,1,3,0:T(8,128)(2,1)} %bitcast.163, bf16[2,80,1280,1]{2,1,0,3:T(8,128)(2,1)S(1)} %bitcast.168), kind=kOutput, calls=%fused_computation.70 | convolution fusion | flops 4037541888 | bytes 40845312 | tf_op jit(solution)/shard_map/bhqk,bkhd->bqhd/dot_general | solution.py:29
  560.3 1.8 copy.25
  562.2 22.6 %fusion.28.clone.5 = bf16[8192,640]{1,0:T(8,128)(2,1)S(1)} fusion(bf16[8192,1280]{1,0:T(8,128)(2,1)} %copy-done.3, f32[640]{0:T(1024)S(1)} %copy-done.17, bf16[2,1280,640]{2,1,0:T(8,128)(2,1)} %param.22), kind=kOutput, calls=%fused_computation.39.clone.clone.clone.2 | convolution fusion | flops 13474201600 | bytes 33098240 | tf_op jit(solution)/shard_map/dot_general | solution.py:32
  584.8 22.1 %fusion.45 = f32[8192,1280]{1,0:T(8,128)} fusion(bf16[2,640,1280]{2,1,0:T(8,128)(2,1)S(1)} %copy-done.23, bf16[8192,640]{1,0:T(8,128)(2,1)S(1)} %fusion.28.clone.5), kind=kOutput, calls=%fused_computation.66 | convolution fusion | flops 13421772800 | bytes 54067200 | tf_op jit(solution)/shard_map/dot_general | solution.py:34
  606.9 20.9 %add_convert_fusion = bf16[8192,1280]{1,0:T(8,128)(2,1)} fusion(f32[8192,1280]{1,0:T(8,128)} %fusion.45, bf16[8192,160]{0,1:T(8,128)(2,1)S(1)} %bitcast.164, bf16[2,160,1280]{2,1,0:T(8,128)(2,1)S(1)} %copy-done.5), kind=kOutput, calls=%fused_computation.17 | convolution fusion | flops 3376414720 | bytes 65945600 | tf_op jit(solution)/shard_map/dot_general | solution.py:31
  627.8 251.4 %all-reduce.5.cloned.1.call-done = bf16[8192,1280]{1,0:T(8,128)(2,1)} async-done(((bf16[8192,1280]{1,0:T(8,128)(2,1)}), bf16[8192,1280]{1,0:T(8,128)(2,1)}) %all-reduce.5.cloned.1.call-update) | async-done | bytes 20971536 | tf_op jit(solution)/shard_map/psum | solution.py:50
  879.3 24.2 %fusion.9 = bf16[8192,1280]{1,0:T(8,128)(2,1)} fusion(bf16[8192,1280]{1,0:T(8,128)(2,1)} %get-tuple-element.14, bf16[8192,1280]{1,0:T(8,128)(2,1)} %all-reduce.5.cloned.1.call-done, f32[1280]{0:T(1024)S(1)} %copy-done.12, f32[1280]{0:T(1024)S(1)} %copy-done.13), kind=kLoop, calls=%fused_computation.12 | loop fusion | flops 62914560 | bytes 62924800 | tf_op jit(solution)/shard_map/convert_element_type | solution.py:52
  (71 shorter events, 9.4 us)
Async XLA Ops:
  6.5 431.4 %all-reduce.3.cloned.1.call-start = ((), (), s32[]{:S(2)}) async-start(), calls=%async_computation | async-start | bytes 41943040 | tf_op jit(solution)/shard_map/psum | solution.py:50
  6.5 15.0 %copy-start = (bf16[32,256,1280]{2,1,0:T(8,128)(2,1)S(1)}, bf16[32,256,1280]{2,1,0:T(8,128)(2,1)}, u32[]{:S(2)}) copy-start(bf16[32,256,1280]{2,1,0:T(8,128)(2,1)} %param.13) | copy-start | bytes 62914564
  9.7 19.6 %copy-start.6 = (bf16[2,1280,160]{1,2,0:T(8,128)(2,1)S(1)}, bf16[2,1280,160]{1,2,0:T(8,128)(2,1)}, u32[]{:S(2)}) copy-start(bf16[2,1280,160]{1,2,0:T(8,128)(2,1)} %param.15) | copy-start | bytes 2457604
  9.7 20.6 %copy-start.7 = (bf16[2,1280,160]{1,2,0:T(8,128)(2,1)S(1)}, bf16[2,1280,160]{1,2,0:T(8,128)(2,1)}, u32[]{:S(2)}) copy-start(bf16[2,1280,160]{1,2,0:T(8,128)(2,1)} %param.16) | copy-start | bytes 2457604
  21.5 9.6 %copy-start.8 = (bf16[2,1280,160]{1,2,0:T(8,128)(2,1)S(1)}, bf16[2,1280,160]{1,2,0:T(8,128)(2,1)}, u32[]{:S(2)}) copy-start(bf16[2,1280,160]{1,2,0:T(8,128)(2,1)} %param.17) | copy-start | bytes 2457604
  39.5 18.8 %copy-start.2 = (bf16[32,256,1280]{2,1,0:T(8,128)(2,1)}, bf16[32,256,1280]{2,1,0:T(8,128)(2,1)S(1)}, u32[]{:S(2)}) copy-start(bf16[32,256,1280]{2,1,0:T(8,128)(2,1)S(1)} %multiply_convert_fusion) | copy-start | bytes 62914564
  49.5 8.8 copy-start.20
  49.5 8.8 copy-start.21
  117.8 23.1 %copy-start.22 = (bf16[2,640,1280]{2,1,0:T(8,128)(2,1)S(1)}, bf16[2,640,1280]{2,1,0:T(8,128)(2,1)}, u32[]{:S(2)}) copy-start(bf16[2,640,1280]{2,1,0:T(8,128)(2,1)} %param.24) | copy-start | bytes 9830404
  140.9 21.8 %copy-start.4 = (bf16[2,160,1280]{2,1,0:T(8,128)(2,1)S(1)}, bf16[2,160,1280]{2,1,0:T(8,128)(2,1)}, u32[]{:S(2)}) copy-start(bf16[2,160,1280]{2,1,0:T(8,128)(2,1)} %param.20) | copy-start | bytes 2457604
  183.7 0.7 copy-start.15
  183.7 0.7 copy-start.16
  183.7 695.6 %all-reduce.5.cloned.1.call-start = ((), (), s32[]{:S(2)}) async-start(), calls=%async_computation.1 | async-start | bytes 41943040 | tf_op jit(solution)/shard_map/psum | solution.py:50
  460.1 17.5 %copy-start.1 = (bf16[8192,1280]{1,0:T(8,128)(2,1)S(1)}, bf16[8192,1280]{1,0:T(8,128)(2,1)}, u32[]{:S(2)}) copy-start(bf16[8192,1280]{1,0:T(8,128)(2,1)} %get-tuple-element.14) | copy-start | bytes 62914564
  460.1 17.5 %copy-start.14 = (f32[1280]{0:T(1024)S(1)}, f32[1280]{0:T(1024)}, u32[]{:S(2)}) copy-start(f32[1280]{0:T(1024)} %get-tuple-element.9) | copy-start | bytes 15364
  477.6 7.7 copy-start.11
  485.3 21.4 %copy-start.3 = (bf16[8192,1280]{1,0:T(8,128)(2,1)}, bf16[8192,1280]{1,0:T(8,128)(2,1)S(1)}, u32[]{:S(2)}) copy-start(bf16[8192,1280]{1,0:T(8,128)(2,1)S(1)} %fusion.6) | copy-start | bytes 62914564
  485.3 12.4 %copy-start.10 = (bf16[1,1280,160]{1,2,0:T(8,128)(2,1)S(1)}, bf16[1,1280,160]{1,2,0:T(8,128)(2,1)}, u32[]{:S(2)}) copy-start(bf16[1,1280,160]{1,2,0:T(8,128)(2,1)} %get-tuple-element.17) | copy-start | bytes 1228804
  497.6 12.7 %copy-start.18 = (f32[80]{0:T(128)S(1)}, f32[80]{0:T(128)}, u32[]{:S(2)}) copy-start(f32[80]{0:T(128)} %get-tuple-element.23) | copy-start | bytes 964
  497.6 12.7 %copy-start.19 = (f32[80]{0:T(128)S(1)}, f32[80]{0:T(128)}, u32[]{:S(2)}) copy-start(f32[80]{0:T(128)} %get-tuple-element.40) | copy-start | bytes 964
  523.2 19.3 %copy-start.9 = (bf16[1,1280,160]{1,2,0:T(8,128)(2,1)S(1)}, bf16[1,1280,160]{1,2,0:T(8,128)(2,1)}, u32[]{:S(2)}) copy-start(bf16[1,1280,160]{1,2,0:T(8,128)(2,1)} %get-tuple-element.15) | copy-start | bytes 1228804
  542.5 19.7 %copy-start.17 = (f32[640]{0:T(1024)S(1)}, f32[640]{0:T(1024)}, u32[]{:S(2)}) copy-start(f32[640]{0:T(1024)} %get-tuple-element.11) | copy-start | bytes 7684
  562.2 22.6 %copy-start.23 = (bf16[2,640,1280]{2,1,0:T(8,128)(2,1)S(1)}, bf16[2,640,1280]{2,1,0:T(8,128)(2,1)}, u32[]{:S(2)}) copy-start(bf16[2,640,1280]{2,1,0:T(8,128)(2,1)} %param.24) | copy-start | bytes 9830404
  584.8 22.1 %copy-start.5 = (bf16[2,160,1280]{2,1,0:T(8,128)(2,1)S(1)}, bf16[2,160,1280]{2,1,0:T(8,128)(2,1)}, u32[]{:S(2)}) copy-start(bf16[2,160,1280]{2,1,0:T(8,128)(2,1)} %param.20) | copy-start | bytes 2457604
  627.8 251.5 %copy-start.12 = (f32[1280]{0:T(1024)S(1)}, f32[1280]{0:T(1024)}, u32[]{:S(2)}) copy-start(f32[1280]{0:T(1024)} %get-tuple-element.7) | copy-start | bytes 15364
  627.8 251.5 %copy-start.13 = (f32[1280]{0:T(1024)S(1)}, f32[1280]{0:T(1024)}, u32[]{:S(2)}) copy-start(f32[1280]{0:T(1024)} %get-tuple-element.42) | copy-start | bytes 15364
Sparse Core Ops, SparseCore 0:
  183.8 254.1 all-reduce.2
  627.9 251.2 all-reduce.4
where the time goes:
time: 919 us; the launch traced here: 911 us
  waiting for transfers between devices  504 us (55%)
  matrix products  226 us (25%)
  other arithmetic  156 us (17%)
  between operations  14.4 us (2%)
  local copies, waits for them, and re-layouts  9.93 us (1%)
    psum x2, waiting for transfers between devices, per_device(): reduced = lax.psum(part_sum.astype(jnp.bfloat16), 'tp')  504 us
    dot_general x2, matrix products, local_branches(): jnp.dot(normed, w_up, preferred_element_type=jnp.float32)  45.7 us
    dot_general x2, matrix products, local_branches(): jnp.dot(activated, w_down, preferred_element_type=jnp.float32)  43.8 us
    dot_general x2, matrix products, local_branches(): attn_part = jnp.dot(mixed_val, w_out, preferred_element_type=jnp.float32)  41.9 us
    reduce_sum x6, other arithmetic, layer_norm(): variance = jnp.mean(centered * centered, axis=-1, keepdims=True)  39.6 us
    sub x2, other arithmetic, local_branches(): attn_prob = jax.nn.softmax(scores, axis=-1).astype(jnp.bfloat16)  38.7 us
    dot_general x4, matrix products, project(): projected = jnp.dot(normed, weight, preferred_element_type=jnp.float32)  36.3 us
    reduce_sum x2, other arithmetic, layer_norm(): mean_val = jnp.mean(values, axis=-1, keepdims=True)  33.9 us
  transfers between devices with their start and end apart: 2, of which 2 were waited for; matrix products, arithmetic and copies ran while one was open for 0% of the time, Pallas kernels for 0%

commit v1 on v0

v1 whole, which is shorter than its diff:
```python
import jax
import jax.numpy as jnp
from jax import lax
from jax.experimental import pallas as pl
from jax.experimental.pallas import tpu as pltpu
from jax.sharding import PartitionSpec as P

LN_EPS = 1e-6
MESH = pl.DeviceIdType.MESH
F32, BF16 = jnp.float32, jnp.bfloat16

IMGS = 8
OWN = 4
SPLIT = 384
PIECES = 8


def normalize(values):
    mean_val = jnp.mean(values, axis=-1, keepdims=True)
    centered = values - mean_val
    variance = jnp.mean(centered * centered, axis=-1, keepdims=True)
    return centered * lax.rsqrt(variance + LN_EPS)


def gelu(pre):
    inner = (2.0 / jnp.pi) ** 0.5 * (pre + 0.044715 * (pre * pre * pre))
    return pre * (0.5 * (1.0 + jnp.tanh(inner)))


def dot(lhs, rhs):
    return jnp.dot(lhs, rhs, preferred_element_type=F32)


def fused(
    tok, wq, wk, wv, wo, w1, w2, ln, qs, ks, bo, bu, b2,
    out, gq, go, g1, g2,
    vq, vo, v1, v2, vb, gain, acc, hid, x1, snd0, rcv0, snd1, rcv1, fin,
    loc0, loc1, xs, s_b, r_b,
    s_c0, r_c0, s_x0, r_x0, s_f0, r_f0,
    s_c1, r_c1, s_y1, r_y1, s_f1, r_f1,
    s_p0, r_p0, s_g0, r_g0, s_p1, r_p1,
    s_out, s_oc, r_oc, s_ox, r_ox, s_oy, r_oy, s_od, r_od,
    s_ex, r_ex, s_ey, r_ey, s_ed, r_ed,
):
    seq, dim = hid.shape[1], hid.shape[2]
    heads_w = wo.shape[1]
    head_dim = qs.shape[1]
    n_heads = heads_w // head_dim
    mlp = w1.shape[2]
    me = lax.axis_index("tp")
    y = me // 4
    x = (me // 2) % 2
    c = me % 2
    cp = me + 1 - 2 * c
    xp = me + 2 - 4 * x
    yp = me + 4 - 8 * y
    xc = xp + 1 - 2 * c
    yc = yp + 1 - 2 * c

    def remote(src, dst, send, recv, dev):
        return pltpu.make_async_remote_copy(
            src_ref=src, dst_ref=dst, send_sem=send, recv_sem=recv,
            device_id={"tp": dev}, device_id_type=MESH)

    def pieces_of(layer):
        return (
            wq.at[layer], wk.at[layer], wv.at[layer], wo.at[layer],
            w1.at[layer, :, pl.ds(0, SPLIT)], w2.at[layer, pl.ds(0, SPLIT), :],
            w1.at[layer, :, pl.ds(SPLIT, mlp - SPLIT)], w2.at[layer, pl.ds(SPLIT, mlp - SPLIT), :],
        )

    def slot_of(refs, slot):
        a, b, d, e = refs
        third = [a.at[slot, pl.ds(n * heads_w, heads_w), :] for n in range(3)]
        return (
            *third, b.at[slot],
            d.at[slot, :, pl.ds(0, SPLIT)], e.at[slot, pl.ds(0, SPLIT), :],
            d.at[slot, :, pl.ds(SPLIT, mlp - SPLIT)], e.at[slot, pl.ds(SPLIT, mlp - SPLIT), :],
        )

    vmem = (vq, vo, v1, v2)
    land = (gq, go, g1, g2)

    def moves(src, dst, send, recv, dev):
        return [remote(src[q], dst[q], send.at[q], recv.at[q], dev) for q in range(PIECES)]

    own_load = [pltpu.make_async_copy(pieces_of(0)[q], slot_of(vmem, 0)[q], loc0.at[q]) for q in range(PIECES)]
    own_core = moves(pieces_of(0), slot_of(vmem, 1), s_c0, r_c0, cp)
    own_x = moves(pieces_of(0), slot_of(vmem, 2), s_x0, r_x0, xp)
    fwd_x = moves(slot_of(vmem, 2), slot_of(vmem, 3), s_f0, r_f0, cp)
    nxt_core = moves(pieces_of(1), slot_of(land, 0), s_c1, r_c1, cp)
    nxt_y = moves(pieces_of(1), slot_of(land, 1), s_y1, r_y1, yp)
    fwd_y = moves(slot_of(land, 1), slot_of(land, 2), s_f1, r_f1, cp)
    peers = (cp, xp, xc, yp, yc)
    biases = [remote(bu, vb.at[n + 1], s_b.at[n], r_b.at[n], peers[n]) for n in range(5)]

    def nxt_load(slot, q):
        src = pieces_of(1) if slot == 0 else slot_of(land, slot - 1)
        return pltpu.make_async_copy(src[q], slot_of(vmem, slot)[q], loc1.at[slot, q])

    group = (2 * x + c) * IMGS

    def image_of(i):
        far = (i < OWN).astype(jnp.int32) if not isinstance(i, int) else int(i < OWN)
        return group + OWN * (y + far - 2 * y * far) + i % OWN

    def load_x(i):
        return pltpu.make_async_copy(tok.at[pl.ds(image_of(i) * seq, seq), :], hid.at[i], xs.at[i])

    for q in range(PIECES):
        own_load[q].start()
    for i in range(IMGS):
        load_x(i).start()

    barrier = pltpu.get_barrier_semaphore()
    for dev in peers:
        pl.semaphore_signal(barrier, inc=1, device_id={"tp": dev}, device_id_type=MESH)
    pl.semaphore_wait(barrier, len(peers))

    for copy in biases:
        copy.start()
    for q in range(PIECES):
        own_x[q].start()
        nxt_y[q].start()
        own_core[q].start()
    for q in range(PIECES):
        nxt_core[q].start()

    def row(ref, layer):
        return ref[layer : layer + 1, :].astype(F32)

    vb[0] = bu[...]
    for layer in range(2):
        for n, ref in enumerate((qs, ks)):
            gain[layer, n] = jnp.broadcast_to(row(ref, layer), (seq, head_dim)).T

    def head_norm(values, layer, n):
        mean_val = jnp.mean(values, axis=0, keepdims=True)
        centered = values - mean_val
        variance = jnp.mean(centered * centered, axis=0, keepdims=True)
        return centered * lax.rsqrt(variance + LN_EPS) * gain[layer, n]

    def attend(i, slot, layer):
        proj = lax.dot_general(vq[slot], hid[i], (((1,), (1,)), ((), ())), preferred_element_type=F32)
        mixed = []
        for hd in range(n_heads):
            lo = hd * head_dim
            q_h = head_norm(proj[lo : lo + head_dim], layer, 0).astype(BF16)
            k_h = head_norm(proj[heads_w + lo : heads_w + lo + head_dim], layer, 1).T.astype(BF16)
            v_h = proj[2 * heads_w + lo : 2 * heads_w + lo + head_dim].astype(BF16)
            scores = dot(k_h, q_h) * head_dim ** -0.5
            weight = jnp.exp(scores - jnp.max(scores, axis=0, keepdims=True))
            total = jnp.sum(weight, axis=0, keepdims=True)
            prob = (weight * (1.0 / total)).astype(BF16)
            mixed.append(dot(v_h, prob))
        mix = jnp.concatenate(mixed, axis=0).T.astype(BF16)
        return dot(mix, vo[slot])

    def mlp_part(i, slot, layer, lo, hi):
        bias = vb[slot + 2 * layer * (slot // 2), layer : layer + 1, lo:hi].astype(F32)
        act = gelu(dot(hid[i], v1[slot, :, lo:hi]) + bias).astype(BF16)
        return dot(act, v2[slot, lo:hi, :])

    @pl.loop(0, IMGS)
    def _(i):
        load_x(i).wait()
        values = hid[i].astype(F32)
        hid[i] = (normalize(values) * row(ln, 0)).astype(BF16)

        @pl.when(i < OWN)
        def _():
            acc[i] = jnp.zeros((seq, dim), F32)

        @pl.when(i >= OWN)
        def _():
            acc[i] = values + row(bo, 0) + row(b2, 0)

    @pl.loop(0, 2)
    def _(slot):
        @pl.when(slot == 0)
        def _():
            for q in range(PIECES):
                own_load[q].wait()
            for copy in biases:
                copy.wait_recv()

        @pl.when(slot == 1)
        def _():
            for q in range(PIECES):
                own_core[q].wait_recv()

        @pl.loop(0, IMGS)
        def _(i):
            acc[i] += attend(i, slot, 0) + mlp_part(i, slot, 0, 0, mlp)

    for q in range(PIECES):
        nxt_core[q].wait_recv()
    for q in range(PIECES):
        nxt_load(0, q).start()
        nxt_load(1, q).start()

    def arrive(slot, pieces):
        @pl.when(slot == 2)
        def _():
            for q in pieces:
                own_x[q].wait_recv()
                fwd_x[q].start()

        @pl.when(slot == 3)
        def _():
            for q in pieces:
                fwd_x[q].wait_recv()

    @pl.loop(2, 4)
    def _(slot):
        arrive(slot, (0, 1, 2, 3))

        @pl.loop(0, IMGS)
        def _(i):
            acc[i] += attend(i, slot, 0)

    @pl.loop(2, 4)
    def _(slot):
        arrive(slot, (4, 5))

        @pl.loop(0, IMGS)
        def _(i):
            acc[i] += mlp_part(i, slot, 0, 0, SPLIT)

    for q in (6, 7):
        own_x[q].wait_recv()
        fwd_x[q].start()
    for q in (6, 7):
        fwd_x[q].wait_recv()

    def part0(k):
        return remote(snd0.at[k], rcv0.at[k], s_p0.at[k], r_p0.at[k], yp)

    def give0(k):
        return remote(x1.at[k], x1.at[OWN + k], s_g0.at[k], r_g0.at[k], xp)

    def part1(k):
        return remote(snd1.at[k], rcv1.at[k], s_p1.at[k], r_p1.at[k], xp)

    @pl.loop(0, IMGS)
    def _(i):
        acc[i] += mlp_part(i, 2, 0, SPLIT, mlp) + mlp_part(i, 3, 0, SPLIT, mlp)

        @pl.when(i < OWN)
        def _():
            snd0[i] = acc[i].astype(BF16)
            part0(i).start()

    for q in range(PIECES):
        nxt_y[q].wait_recv()
        fwd_y[q].start()
    for q in range(PIECES):
        fwd_x[q].wait_send()
    for q in range(PIECES):
        nxt_load(2, q).start()
    for q in range(PIECES):
        fwd_y[q].wait_recv()
    for q in range(PIECES):
        nxt_load(3, q).start()

    def layer1(src, finish):
        values = x1[src].astype(F32)
        hid[0] = (normalize(values) * row(ln, 1)).astype(BF16)
        if finish:
            acc[0] = values + row(bo, 1) + row(b2, 1)
        else:
            acc[0] = jnp.zeros((seq, dim), F32)

        @pl.loop(0, 4)
        def _(slot):
            acc[0] += attend(0, slot, 1) + mlp_part(0, slot, 1, 0, mlp)

    def rows_of(chip_x, chip_y, core, k):
        return pl.ds(((2 * (1 - chip_x) + core) * IMGS + OWN * chip_y + k) * seq, seq)

    def put(k):
        rows = rows_of(x, y, c, k)
        return (
            pltpu.make_async_copy(fin.at[k], out.at[rows, :], s_out.at[k]),
            remote(fin.at[k], out.at[rows, :], s_oc.at[k], r_oc.at[k], cp),
            remote(fin.at[k], out.at[rows, :], s_ox.at[k], r_ox.at[k], xp),
            remote(fin.at[k], out.at[rows, :], s_oy.at[k], r_oy.at[k], yp),
        )

    def pass_on(k):
        of_x = out.at[rows_of(1 - x, y, c, k), :]
        of_y = out.at[rows_of(x, 1 - y, c, k), :]
        of_d = out.at[rows_of(1 - x, 1 - y, c, k), :]
        return (
            remote(of_x, of_x, s_od.at[k], r_od.at[k], yp),
            remote(of_x, of_x, s_ex.at[k], r_ex.at[k], cp),
            remote(of_y, of_y, s_ey.at[k], r_ey.at[k], cp),
            remote(of_d, of_d, s_ed.at[k], r_ed.at[k], cp),
        )

    def come(k):
        of_c = out.at[rows_of(x, y, 1 - c, k), :]
        of_x = out.at[rows_of(1 - x, y, c, k), :]
        of_y = out.at[rows_of(x, 1 - y, c, k), :]
        of_d = out.at[rows_of(1 - x, 1 - y, c, k), :]
        of_cx = out.at[rows_of(1 - x, y, 1 - c, k), :]
        of_cy = out.at[rows_of(x, 1 - y, 1 - c, k), :]
        of_cd = out.at[rows_of(1 - x, 1 - y, 1 - c, k), :]
        return (
            remote(of_c, of_c, s_oc.at[k], r_oc.at[k], cp),
            remote(of_x, of_x, s_ox.at[k], r_ox.at[k], xp),
            remote(of_y, of_y, s_oy.at[k], r_oy.at[k], yp),
            remote(of_d, of_d, s_od.at[k], r_od.at[k], yp),
            remote(of_cx, of_cx, s_ex.at[k], r_ex.at[k], cp),
            remote(of_cy, of_cy, s_ey.at[k], r_ey.at[k], cp),
            remote(of_cd, of_cd, s_ed.at[k], r_ed.at[k], cp),
        )

    def near(k):
        part0(k).wait_recv()
        x1[k] = (acc[OWN + k] + rcv0[k].astype(F32)).astype(BF16)
        give0(k).start()

    def near_layer1(k):
        layer1(k, False)
        snd1[k] = acc[0].astype(BF16)
        part1(k).start()

    def far(k):
        give0(k).wait_recv()
        layer1(OWN + k, True)
        part1(k).wait_recv()
        fin[k] = (acc[0] + rcv1[k].astype(F32)).astype(BF16)
        for copy in put(k):
            copy.start()

    @pl.loop(0, OWN)
    def _(k):
        near(k)

        @pl.when(k == 0)
        def _():
            for slot in range(4):
                for q in range(PIECES):
                    nxt_load(slot, q).wait()

        near_layer1(k)

        @pl.when(k >= 1)
        def _():
            far(k - 1)

    far(OWN - 1)

    @pl.loop(0, OWN)
    def _(k):
        to_d, to_cx, to_cy, _ = pass_on(k)
        _, by_x, by_y, _, _, _, _ = come(k)
        by_y.wait_recv()
        to_cy.start()
        by_x.wait_recv()
        to_d.start()
        to_cx.start()

    @pl.loop(0, OWN)
    def _(k):
        come(k)[3].wait_recv()
        pass_on(k)[3].start()

    @pl.loop(0, OWN)
    def _(k):
        by_c, _, _, _, by_cx, by_cy, by_cd = come(k)
        for copy in (by_c, by_cx, by_cy, by_cd):
            copy.wait_recv()
        local, *others = put(k)
        local.wait()
        for copy in (*others, *pass_on(k), part0(k), give0(k), part1(k)):
            copy.wait_send()

    for copy in biases:
        copy.wait_send()
    for q in range(PIECES):
        own_core[q].wait_send()
        own_x[q].wait_send()
        nxt_core[q].wait_send()
        nxt_y[q].wait_send()
        fwd_y[q].wait_send()


def solution(mesh):
    col_spec = P(None, None, "tp")
    row_spec = P(None, "tp", None)
    in_specs = (P("dp", None, None), P(), col_spec, col_spec, col_spec, P(), P(), row_spec, P(), col_spec, P(None, "tp"), row_spec, P())

    def per_device(tokens_in, ln_scale, w_query, w_key, w_value, q_scale, k_scale, w_out, b_out, w_up, b_up, w_down, b_down):
        n_images, seq, dim = tokens_in.shape
        layers, _, heads_w = w_query.shape
        mlp = w_up.shape[2]
        across = lambda w: jnp.swapaxes(w, 1, 2)
        any_spec = pl.BlockSpec(memory_space=pl.ANY)
        vm_spec = pl.BlockSpec(memory_space=pltpu.VMEM)
        dma = lambda *shape: pltpu.SemaphoreType.DMA(shape)
        shape = jax.ShapeDtypeStruct
        encoded, *_ = pl.pallas_call(
            fused,
            out_shape=(
                shape((n_images * seq, dim), BF16),
                shape((3, 3 * heads_w, dim), BF16),
                shape((3, heads_w, dim), BF16),
                shape((3, dim, mlp), BF16),
                shape((3, mlp, dim), BF16),
            ),
            in_specs=[any_spec] * 7 + [vm_spec] * 6,
            out_specs=(any_spec,) * 5,
            scratch_shapes=[
                pltpu.VMEM((4, 3 * heads_w, dim), BF16),
                pltpu.VMEM((4, heads_w, dim), BF16),
                pltpu.VMEM((4, dim, mlp), BF16),
                pltpu.VMEM((4, mlp, dim), BF16),
                pltpu.VMEM((6, layers, mlp), BF16),
                pltpu.VMEM((layers, 2, q_scale.shape[1], seq), F32),
                pltpu.VMEM((IMGS, seq, dim), F32),
                pltpu.VMEM((IMGS, seq, dim), BF16),
                pltpu.VMEM((IMGS, seq, dim), BF16),
                *[pltpu.VMEM((OWN, seq, dim), BF16)] * 5,
                dma(PIECES), dma(4, PIECES), dma(IMGS), dma(5), dma(5),
                *[dma(PIECES)] * 12,
                *[dma(OWN)] * 6,
                *[dma(OWN)] * 9,
                *[dma(OWN)] * 6,
            ],
            compiler_params=pltpu.CompilerParams(
                collective_id=0, has_side_effects=True, vmem_limit_bytes=67000000),
        )(tokens_in.reshape(n_images * seq, dim), across(w_query), across(w_key), across(w_value), w_out, w_up, w_down, ln_scale, q_scale, k_scale, b_out, b_up, b_down)
        return encoded.reshape(n_images, seq, dim)

    return jax.shard_map(per_device, mesh=mesh, in_specs=in_specs, out_specs=P("dp", None, None), check_vma=False)
```

time: 919 us -> 367 us (0.40)
  waiting for transfers between devices: 504 us -> 0 us
  Pallas kernels: 0 us -> 349 us
  matrix products: 226 us -> 0 us
  other arithmetic: 156 us -> 0 us
  between operations: 14.4 us -> 0.01 us
    psum x2 -> x0, waiting for transfers between devices: 504 us -> none  [per_device(): reduced = lax.psum(part_sum.astype(jnp.bfloat16), 'tp')]
    pallas_call x0 -> x1, Pallas kernels: none -> 349 us  [per_device(): pl.pallas_call(fused, out_shape=(shape((n_images * seq, dim), BF16), shap...]
    dot_general x14 -> x0, matrix products: 226 us -> none  [the longest x2 45.7 us: local_branches(): jnp.dot(normed, w_up, preferred_element_type=jnp.float32)]
    reduce_sum x8 -> x0, other arithmetic: 73.5 us -> none  [the longest x6 39.6 us: layer_norm(): variance = jnp.mean(centered * centered, axis=-1, keepdims=True)]
    convert_element_type x4 -> x0, other arithmetic: 40 us -> none  [the longest x1 24.2 us: per_device(): current = summed.astype(jnp.bfloat16).reshape(n_images, seq_len, model_dim)]
    sub x2 -> x0, other arithmetic: 38.7 us -> none  [local_branches(): attn_prob = jax.nn.softmax(scores, axis=-1).astype(jnp.bfloat16)]
    unnamed x50 -> x1, local copies, waits for them, and re-layouts: 4.39 us -> 17.4 us
  transfers between devices with their start and end apart: 2 -> 0, of which waited for: 2 -> 0; matrix products, arithmetic and copies ran while one was open for 0% -> 0% of each run, Pallas kernels for 0% -> 0%
where the time goes in v1:
time: 367 us
  Pallas kernels  349 us (95%)
  local copies, waits for them, and re-layouts  17.4 us (5%)
    pallas_call x1, Pallas kernels, per_device(): pl.pallas_call(fused, out_shape=(shape((n_images * seq, dim), BF16), shap...  349 us
    unnamed x1, local copies, waits for them, and re-layouts  17.4 us

profile of v1, /device:TPU:0, one launch (start us, length us, event | category | flops | bytes accessed | tf_op | source)
XLA Modules:
  0.0 366.8 jit_solution(12404017077309510025)
XLA Ops:
  0.0 349.4 %shard_map.127 = (bf16[8192,1280]{1,0:T(8,128)(2,1)}, bf16[3,480,1280]{2,1,0:T(8,128)(2,1)}, bf16[3,160,1280]{2,1,0:T(8,128)(2,1)}, bf16[3,1280,640]{2,1,0:T(8,128)(2,1)}, bf16[3,640,1280]{2,1,0:T(8,128)(2,1)}) custom-call(bf16[8192,1280]{1,0:T(8,128)(2,1)} %bitcast.6, bf16[2,160,1280]{2,1,0:T(8,128)(2,1)} %bitcast.7, bf16[2,160,1280]{2,1,0:T(8,128)(2,1)} %bitcast.8, ...), custom_call_target="tpu_custom_call" | custom-call | tf_op jit(solution)/shard_map/pallas_call | solution.py:404
  349.4 17.4 %copy.15 = bf16[32,256,1280]{2,1,0:T(8,128)(2,1)} copy(bf16[32,256,1280]{2,1,0:T(8,128)(2,1)} %bitcast.5) | data formatting | bytes 41943040

commit v2 on v1

--- a/solution.py
+++ b/solution.py
@@ -13,6 +13,8 @@
 OWN = 4
 SPLIT = 384
 PIECES = 8
+CUTS = 4
+HALVES = 2
 
 
 def normalize(values):
@@ -107,14 +109,13 @@
     def load_x(i):
         return pltpu.make_async_copy(tok.at[pl.ds(image_of(i) * seq, seq), :], hid.at[i], xs.at[i])
 
+    barrier = pltpu.get_barrier_semaphore()
+    for dev in peers:
+        pl.semaphore_signal(barrier, inc=1, device_id={"tp": dev}, device_id_type=MESH)
     for q in range(PIECES):
         own_load[q].start()
     for i in range(IMGS):
         load_x(i).start()
-
-    barrier = pltpu.get_barrier_semaphore()
-    for dev in peers:
-        pl.semaphore_signal(barrier, inc=1, device_id={"tp": dev}, device_id_type=MESH)
     pl.semaphore_wait(barrier, len(peers))
 
     for copy in biases:
@@ -219,6 +220,10 @@
         def _(i):
             acc[i] += attend(i, slot, 0)
 
+    for q in range(4):
+        nxt_y[q].wait_recv()
+        fwd_y[q].start()
+
     @pl.loop(2, 4)
     def _(slot):
         arrive(slot, (4, 5))
@@ -226,6 +231,10 @@
         @pl.loop(0, IMGS)
         def _(i):
             acc[i] += mlp_part(i, slot, 0, 0, SPLIT)
+
+    for q in (4, 5):
+        nxt_y[q].wait_recv()
+        fwd_y[q].start()
 
     for q in (6, 7):
         own_x[q].wait_recv()
@@ -233,11 +242,14 @@
     for q in (6, 7):
         fwd_x[q].wait_recv()
 
-    def part0(k):
-        return remote(snd0.at[k], rcv0.at[k], s_p0.at[k], r_p0.at[k], yp)
-
-    def give0(k):
-        return remote(x1.at[k], x1.at[OWN + k], s_g0.at[k], r_g0.at[k], xp)
+    def cut(n):
+        return pl.ds(n * (seq // CUTS), seq // CUTS)
+
+    def part0(k, n):
+        return remote(snd0.at[k, cut(n), :], rcv0.at[k, cut(n), :], s_p0.at[k, n], r_p0.at[k, n], yp)
+
+    def give0(k, n):
+        return remote(x1.at[k, cut(n), :], x1.at[OWN + k, cut(n), :], s_g0.at[k, n], r_g0.at[k, n], xp)
 
     def part1(k):
         return remote(snd1.at[k], rcv1.at[k], s_p1.at[k], r_p1.at[k], xp)
@@ -249,9 +261,10 @@
         @pl.when(i < OWN)
         def _():
             snd0[i] = acc[i].astype(BF16)
-            part0(i).start()
-
-    for q in range(PIECES):
+            for n in range(CUTS):
+                part0(i, n).start()
+
+    for q in (6, 7):
         nxt_y[q].wait_recv()
         fwd_y[q].start()
     for q in range(PIECES):
@@ -275,51 +288,50 @@
         def _(slot):
             acc[0] += attend(0, slot, 1) + mlp_part(0, slot, 1, 0, mlp)
 
-    def rows_of(chip_x, chip_y, core, k):
-        return pl.ds(((2 * (1 - chip_x) + core) * IMGS + OWN * chip_y + k) * seq, seq)
-
-    def put(k):
-        rows = rows_of(x, y, c, k)
+    def half_of(chip_x, chip_y, core, k, n):
+        image = (2 * (1 - chip_x) + core) * IMGS + OWN * chip_y + k
+        return out.at[pl.ds(image * seq + n * (seq // HALVES), seq // HALVES), :]
+
+    def put(k, n):
+        src = fin.at[k, pl.ds(n * (seq // HALVES), seq // HALVES), :]
+        dst = half_of(x, y, c, k, n)
         return (
-            pltpu.make_async_copy(fin.at[k], out.at[rows, :], s_out.at[k]),
-            remote(fin.at[k], out.at[rows, :], s_oc.at[k], r_oc.at[k], cp),
-            remote(fin.at[k], out.at[rows, :], s_ox.at[k], r_ox.at[k], xp),
-            remote(fin.at[k], out.at[rows, :], s_oy.at[k], r_oy.at[k], yp),
+            pltpu.make_async_copy(src, dst, s_out.at[k, n]),
+            remote(src, dst, s_oc.at[k, n], r_oc.at[k, n], cp),
+            remote(src, dst, s_oy.at[k, n], r_oy.at[k, n], yp),
+            remote(src, dst, s_ox.at[k, n], r_ox.at[k, n], xp),
         )
 
-    def pass_on(k):
-        of_x = out.at[rows_of(1 - x, y, c, k), :]
-        of_y = out.at[rows_of(x, 1 - y, c, k), :]
-        of_d = out.at[rows_of(1 - x, 1 - y, c, k), :]
+    def pass_on(k, n):
+        of_x = half_of(1 - x, y, c, k, n)
+        of_y = half_of(x, 1 - y, c, k, n)
+        of_d = half_of(1 - x, 1 - y, c, k, n)
         return (
-            remote(of_x, of_x, s_od.at[k], r_od.at[k], yp),
-            remote(of_x, of_x, s_ex.at[k], r_ex.at[k], cp),
-            remote(of_y, of_y, s_ey.at[k], r_ey.at[k], cp),
-            remote(of_d, of_d, s_ed.at[k], r_ed.at[k], cp),
+            remote(of_x, of_x, s_od.at[k, n], r_od.at[k, n], yp),
+            remote(of_x, of_x, s_ex.at[k, n], r_ex.at[k, n], cp),
+            remote(of_y, of_y, s_ey.at[k, n], r_ey.at[k, n], cp),
+            remote(of_d, of_d, s_ed.at[k, n], r_ed.at[k, n], cp),
         )
 
-    def come(k):
-        of_c = out.at[rows_of(x, y, 1 - c, k), :]
-        of_x = out.at[rows_of(1 - x, y, c, k), :]
-        of_y = out.at[rows_of(x, 1 - y, c, k), :]
-        of_d = out.at[rows_of(1 - x, 1 - y, c, k), :]
-        of_cx = out.at[rows_of(1 - x, y, 1 - c, k), :]
-        of_cy = out.at[rows_of(x, 1 - y, 1 - c, k), :]
-        of_cd = out.at[rows_of(1 - x, 1 - y, 1 - c, k), :]
+    def come(k, n):
+        def into(ref, recv):
+            return remote(ref, ref, s_out.at[k, n], recv.at[k, n], cp)
+
         return (
-            remote(of_c, of_c, s_oc.at[k], r_oc.at[k], cp),
-            remote(of_x, of_x, s_ox.at[k], r_ox.at[k], xp),
-            remote(of_y, of_y, s_oy.at[k], r_oy.at[k], yp),
-            remote(of_d, of_d, s_od.at[k], r_od.at[k], yp),
-            remote(of_cx, of_cx, s_ex.at[k], r_ex.at[k], cp),
-            remote(of_cy, of_cy, s_ey.at[k], r_ey.at[k], cp),
-            remote(of_cd, of_cd, s_ed.at[k], r_ed.at[k], cp),
+            into(half_of(1 - x, y, c, k, n), r_ox),
+            into(half_of(x, 1 - y, c, k, n), r_oy),
+            into(half_of(1 - x, 1 - y, c, k, n), r_od),
+            into(half_of(x, y, 1 - c, k, n), r_oc),
+            into(half_of(1 - x, y, 1 - c, k, n), r_ex),
+            into(half_of(x, 1 - y, 1 - c, k, n), r_ey),
+            into(half_of(1 - x, 1 - y, 1 - c, k, n), r_ed),
         )
 
     def near(k):
-        part0(k).wait_recv()
-        x1[k] = (acc[OWN + k] + rcv0[k].astype(F32)).astype(BF16)
-        give0(k).start()
+        for n in range(CUTS):
+            part0(k, n).wait_recv()
+            x1[k, cut(n), :] = (acc[OWN + k, cut(n), :] + rcv0[k, cut(n), :].astype(F32)).astype(BF16)
+            give0(k, n).start()
 
     def near_layer1(k):
         layer1(k, False)
@@ -327,55 +339,79 @@
         part1(k).start()
 
     def far(k):
-        give0(k).wait_recv()
+        for n in range(CUTS):
+            give0(k, n).wait_recv()
         layer1(OWN + k, True)
         part1(k).wait_recv()
         fin[k] = (acc[0] + rcv1[k].astype(F32)).astype(BF16)
-        for copy in put(k):
-            copy.start()
+        for n in range(HALVES):
+            for copy in put(k, n)[:3]:
+                copy.start()
+
+    def far_x(k):
+        for n in range(HALVES):
+            put(k, n)[3].start()
+
+    near(0)
+    for slot in range(4):
+        for q in range(PIECES):
+            nxt_load(slot, q).wait()
 
     @pl.loop(0, OWN)
     def _(k):
-        near(k)
-
-        @pl.when(k == 0)
-        def _():
-            for slot in range(4):
-                for q in range(PIECES):
-                    nxt_load(slot, q).wait()
-
         near_layer1(k)
 
+        @pl.when(k < OWN - 1)
+        def _():
+            near(k + 1)
+
+        @pl.when(k == OWN - 1)
+        def _():
+            for early in range(OWN - 2):
+                far_x(early)
+
         @pl.when(k >= 1)
         def _():
             far(k - 1)
 
+    far_x(OWN - 2)
     far(OWN - 1)
+    far_x(OWN - 1)
+
+    lag = 2
+
+    @pl.loop(0, OWN * HALVES + lag)
+    def _(j):
+        @pl.when(j < OWN * HALVES)
+        def _():
+            k, n = j // HALVES, j % HALVES
+            by_x, by_y, *_ = come(k, n)
+            to_d, x_core, y_core, _ = pass_on(k, n)
+            by_y.wait_recv()
+            y_core.start()
+            by_x.wait_recv()
+            to_d.start()
+            x_core.start()
+
+        @pl.when(j >= lag)
+        def _():
+            k, n = (j - lag) // HALVES, (j - lag) % HALVES
+            come(k, n)[2].wait_recv()
+            pass_on(k, n)[3].start()
 
     @pl.loop(0, OWN)
     def _(k):
-        to_d, to_cx, to_cy, _ = pass_on(k)
-        _, by_x, by_y, _, _, _, _ = come(k)
-        by_y.wait_recv()
-        to_cy.start()
-        by_x.wait_recv()
-        to_d.start()
-        to_cx.start()
-
-    @pl.loop(0, OWN)
-    def _(k):
-        come(k)[3].wait_recv()
-        pass_on(k)[3].start()
-
-    @pl.loop(0, OWN)
-    def _(k):
-        by_c, _, _, _, by_cx, by_cy, by_cd = come(k)
-        for copy in (by_c, by_cx, by_cy, by_cd):
-            copy.wait_recv()
-        local, *others = put(k)
-        local.wait()
-        for copy in (*others, *pass_on(k), part0(k), give0(k), part1(k)):
-            copy.wait_send()
+        part1(k).wait_send()
+        for n in range(CUTS):
+            part0(k, n).wait_send()
+            give0(k, n).wait_send()
+        for n in range(HALVES):
+            local, *others = put(k, n)
+            local.wait()
+            for copy in (*others, *pass_on(k, n)):
+                copy.wait_send()
+            for copy in come(k, n)[3:]:
+                copy.wait_recv()
 
     for copy in biases:
         copy.wait_send()
@@ -425,9 +461,8 @@
                 *[pltpu.VMEM((OWN, seq, dim), BF16)] * 5,
                 dma(PIECES), dma(4, PIECES), dma(IMGS), dma(5), dma(5),
                 *[dma(PIECES)] * 12,
-                *[dma(OWN)] * 6,
-                *[dma(OWN)] * 9,
-                *[dma(OWN)] * 6,
+                *[dma(OWN, CUTS)] * 4, dma(OWN), dma(OWN),
+                *[dma(OWN, HALVES)] * 15,
             ],
             compiler_params=pltpu.CompilerParams(
                 collective_id=0, has_side_effects=True, vmem_limit_bytes=67000000),

time: 367 us -> 337 us (0.918)
  Pallas kernels: 349 us -> 319 us
    pallas_call x1, Pallas kernels: 349 us -> 319 us  [per_device(): pl.pallas_call(fused, out_shape=(shape((n_images * seq, dim), BF16), shap...]
where the time goes in v2:
time: 337 us
  Pallas kernels  319 us (95%)
  local copies, waits for them, and re-layouts  17.4 us (5%)
    pallas_call x1, Pallas kernels, per_device(): pl.pallas_call(fused, out_shape=(shape((n_images * seq, dim), BF16), shap...  319 us
    unnamed x1, local copies, waits for them, and re-layouts  17.4 us

profile of v2, /device:TPU:0, one launch (start us, length us, event | category | flops | bytes accessed | tf_op | source)
XLA Modules:
  0.0 336.6 jit_solution(17374591397670664208)
XLA Ops:
  0.0 319.3 %shard_map.127 = (bf16[8192,1280]{1,0:T(8,128)(2,1)}, bf16[3,480,1280]{2,1,0:T(8,128)(2,1)}, bf16[3,160,1280]{2,1,0:T(8,128)(2,1)}, bf16[3,1280,640]{2,1,0:T(8,128)(2,1)}, bf16[3,640,1280]{2,1,0:T(8,128)(2,1)}) custom-call(bf16[8192,1280]{1,0:T(8,128)(2,1)} %bitcast.6, bf16[2,160,1280]{2,1,0:T(8,128)(2,1)} %bitcast.7, bf16[2,160,1280]{2,1,0:T(8,128)(2,1)} %bitcast.8, ...), custom_call_target="tpu_custom_call" | custom-call | tf_op jit(solution)/shard_map/pallas_call | solution.py:440
  319.3 17.4 %copy.15 = bf16[32,256,1280]{2,1,0:T(8,128)(2,1)} copy(bf16[32,256,1280]{2,1,0:T(8,128)(2,1)} %bitcast.5) | data formatting | bytes 41943040

commit v3 on v2

--- a/solution.py
+++ b/solution.py
@@ -14,7 +14,8 @@
 SPLIT = 384
 PIECES = 8
 CUTS = 4
-HALVES = 2
+PARTS = 4
+TURN = 14
 
 
 def normalize(values):
@@ -36,13 +37,13 @@
 def fused(
     tok, wq, wk, wv, wo, w1, w2, ln, qs, ks, bo, bu, b2,
     out, gq, go, g1, g2,
-    vq, vo, v1, v2, vb, gain, acc, hid, x1, snd0, rcv0, snd1, rcv1, fin,
+    vq, vo, v1, v2, vb, gain, acc, hid, x1,
     loc0, loc1, xs, s_b, r_b,
     s_c0, r_c0, s_x0, r_x0, s_f0, r_f0,
     s_c1, r_c1, s_y1, r_y1, s_f1, r_f1,
     s_p0, r_p0, s_g0, r_g0, s_p1, r_p1,
-    s_out, s_oc, r_oc, s_ox, r_ox, s_oy, r_oy, s_od, r_od,
-    s_ex, r_ex, s_ey, r_ey, s_ed, r_ed,
+    s_oc, r_oc, s_ey, r_ey,
+    s_ox, r_ox, s_oy, r_oy, s_od, r_od, s_ex, r_ex, s_ed, r_ed,
 ):
     seq, dim = hid.shape[1], hid.shape[2]
     heads_w = wo.shape[1]
@@ -245,14 +246,20 @@
     def cut(n):
         return pl.ds(n * (seq // CUTS), seq // CUTS)
 
-    def part0(k, n):
-        return remote(snd0.at[k, cut(n), :], rcv0.at[k, cut(n), :], s_p0.at[k, n], r_p0.at[k, n], yp)
+    def rows_of(chip_x, chip_y, core, k):
+        return ((2 * (1 - chip_x) + core) * IMGS + OWN * chip_y + k) * seq
+
+    def lent(chip_y, k, n):
+        return pl.ds(pl.multiple_of(rows_of(1 - x, chip_y, c, k) + n * (seq // CUTS), seq // CUTS), seq // CUTS)
+
+    def part0(k, n, chip_y):
+        return remote(hid.at[k, cut(n), :], out.at[lent(chip_y, k, n), :], s_p0.at[k, n], r_p0.at[k, n], yp)
 
     def give0(k, n):
-        return remote(x1.at[k, cut(n), :], x1.at[OWN + k, cut(n), :], s_g0.at[k, n], r_g0.at[k, n], xp)
-
-    def part1(k):
-        return remote(snd1.at[k], rcv1.at[k], s_p1.at[k], r_p1.at[k], xp)
+        return remote(out.at[lent(y, k, n), :], x1.at[k, cut(n), :], s_g0.at[k, n], r_g0.at[k, n], xp)
+
+    def part1(k, chip_x):
+        return remote(hid.at[OWN + k], out.at[pl.ds(rows_of(chip_x, y, c, k), seq), :], s_p1.at[k], r_p1.at[k], xp)
 
     @pl.loop(0, IMGS)
     def _(i):
@@ -260,9 +267,9 @@
 
         @pl.when(i < OWN)
         def _():
-            snd0[i] = acc[i].astype(BF16)
+            hid[i] = acc[i].astype(BF16)
             for n in range(CUTS):
-                part0(i, n).start()
+                part0(i, n, 1 - y).start()
 
     for q in (6, 7):
         nxt_y[q].wait_recv()
@@ -276,8 +283,8 @@
     for q in range(PIECES):
         nxt_load(3, q).start()
 
-    def layer1(src, finish):
-        values = x1[src].astype(F32)
+    def layer1(values, finish, between=None):
+        values = values.astype(F32)
         hid[0] = (normalize(values) * row(ln, 1)).astype(BF16)
         if finish:
             acc[0] = values + row(bo, 1) + row(b2, 1)
@@ -287,72 +294,125 @@
         @pl.loop(0, 4)
         def _(slot):
             acc[0] += attend(0, slot, 1) + mlp_part(0, slot, 1, 0, mlp)
-
-    def half_of(chip_x, chip_y, core, k, n):
-        image = (2 * (1 - chip_x) + core) * IMGS + OWN * chip_y + k
-        return out.at[pl.ds(image * seq + n * (seq // HALVES), seq // HALVES), :]
+            if between is not None:
+                between(slot)
+
+    def part_of(chip_x, chip_y, core, k, n):
+        return out.at[pl.ds(rows_of(chip_x, chip_y, core, k) + n * (seq // PARTS), seq // PARTS), :]
+
+    def image_at(chip_x, chip_y, core, k):
+        return out.at[pl.ds(rows_of(chip_x, chip_y, core, k), seq), :]
+
+    def put_core(k):
+        ref = image_at(x, y, c, k)
+        return remote(ref, ref, s_oc.at[k], r_oc.at[k], cp)
+
+    def pass_y(k):
+        ref = image_at(x, 1 - y, c, k)
+        return remote(ref, ref, s_ey.at[k], r_ey.at[k], cp)
+
+    def come_core(k):
+        own, of_y = image_at(x, y, 1 - c, k), image_at(x, 1 - y, 1 - c, k)
+        return (
+            remote(own, own, s_oc.at[k], r_oc.at[k], cp),
+            remote(of_y, of_y, s_ey.at[k], r_ey.at[k], cp),
+        )
 
     def put(k, n):
-        src = fin.at[k, pl.ds(n * (seq // HALVES), seq // HALVES), :]
-        dst = half_of(x, y, c, k, n)
+        ref = part_of(x, y, c, k, n)
         return (
-            pltpu.make_async_copy(src, dst, s_out.at[k, n]),
-            remote(src, dst, s_oc.at[k, n], r_oc.at[k, n], cp),
-            remote(src, dst, s_oy.at[k, n], r_oy.at[k, n], yp),
-            remote(src, dst, s_ox.at[k, n], r_ox.at[k, n], xp),
+            remote(ref, ref, s_oy.at[k, n], r_oy.at[k, n], yp),
+            remote(ref, ref, s_ox.at[k, n], r_ox.at[k, n], xp),
         )
 
     def pass_on(k, n):
-        of_x = half_of(1 - x, y, c, k, n)
-        of_y = half_of(x, 1 - y, c, k, n)
-        of_d = half_of(1 - x, 1 - y, c, k, n)
+        of_x = part_of(1 - x, y, c, k, n)
+        of_y = part_of(x, 1 - y, c, k, n)
+        of_d = part_of(1 - x, 1 - y, c, k, n)
         return (
             remote(of_x, of_x, s_od.at[k, n], r_od.at[k, n], yp),
+            remote(of_y, of_y, s_od.at[k, n], r_od.at[k, n], xp),
             remote(of_x, of_x, s_ex.at[k, n], r_ex.at[k, n], cp),
-            remote(of_y, of_y, s_ey.at[k, n], r_ey.at[k, n], cp),
             remote(of_d, of_d, s_ed.at[k, n], r_ed.at[k, n], cp),
         )
 
     def come(k, n):
         def into(ref, recv):
-            return remote(ref, ref, s_out.at[k, n], recv.at[k, n], cp)
+            return remote(ref, ref, s_ox.at[k, n], recv.at[k, n], cp)
 
         return (
-            into(half_of(1 - x, y, c, k, n), r_ox),
-            into(half_of(x, 1 - y, c, k, n), r_oy),
-            into(half_of(1 - x, 1 - y, c, k, n), r_od),
-            into(half_of(x, y, 1 - c, k, n), r_oc),
-            into(half_of(1 - x, y, 1 - c, k, n), r_ex),
-            into(half_of(x, 1 - y, 1 - c, k, n), r_ey),
-            into(half_of(1 - x, 1 - y, 1 - c, k, n), r_ed),
+            into(part_of(1 - x, y, c, k, n), r_ox),
+            into(part_of(x, 1 - y, c, k, n), r_oy),
+            into(part_of(1 - x, 1 - y, c, k, n), r_od),
+            into(part_of(1 - x, y, 1 - c, k, n), r_ex),
+            into(part_of(1 - x, 1 - y, 1 - c, k, n), r_ed),
         )
 
-    def near(k):
+    def near(k, n):
+        part0(k, n, y).wait_recv()
+        rows = lent(y, k, n)
+        out[rows, :] = (acc[OWN + k, cut(n), :] + out[rows, :].astype(F32)).astype(BF16)
+        give0(k, n).start()
+
+    def near_behind(k, when):
+        def between(slot):
+            @pl.when(when & (slot >= 1))
+            def _():
+                near(k, slot - 1)
+
+        def rest():
+            @pl.when(when)
+            def _():
+                near(k, CUTS - 1)
+
+        return between, rest
+
+    def near_layer1(k):
+        between, rest = near_behind(k + 1, k < OWN - 2)
+        rows = pl.ds(pl.multiple_of(rows_of(1 - x, y, c, k), seq), seq)
+        layer1(out[rows, :], False, between)
+        hid[OWN + k] = acc[0].astype(BF16)
         for n in range(CUTS):
-            part0(k, n).wait_recv()
-            x1[k, cut(n), :] = (acc[OWN + k, cut(n), :] + rcv0[k, cut(n), :].astype(F32)).astype(BF16)
-            give0(k, n).start()
-
-    def near_layer1(k):
-        layer1(k, False)
-        snd1[k] = acc[0].astype(BF16)
-        part1(k).start()
-
-    def far(k):
+            give0(k, n).wait_send()
+        part1(k, 1 - x).start()
+        rest()
+
+    def far(k, before=None):
         for n in range(CUTS):
             give0(k, n).wait_recv()
-        layer1(OWN + k, True)
-        part1(k).wait_recv()
-        fin[k] = (acc[0] + rcv1[k].astype(F32)).astype(BF16)
-        for n in range(HALVES):
-            for copy in put(k, n)[:3]:
+        if before is None:
+            between, rest = near_behind(OWN - 1, k == 0)
+            layer1(x1[k], True, between)
+            rest()
+        else:
+            layer1(x1[k], True)
+            before()
+        part1(k, x).wait_recv()
+        rows = pl.ds(pl.multiple_of(rows_of(x, y, c, k), seq), seq)
+        out[rows, :] = (acc[0] + out[rows, :].astype(F32)).astype(BF16)
+        put_core(k).start()
+        for n in range(PARTS):
+            for copy in put(k, n):
                 copy.start()
 
-    def far_x(k):
-        for n in range(HALVES):
-            put(k, n)[3].start()
-
-    near(0)
+    def pass_x(k, n):
+        come(k, n)[0].wait_recv()
+        to_d, _, x_core, _ = pass_on(k, n)
+
+        @pl.when(k * PARTS + n < TURN)
+        def _():
+            to_d.start()
+
+        x_core.start()
+
+    def pass_x_all(k):
+        for n in range(PARTS):
+            pass_x(k, n)
+
+    for n in range(CUTS):
+        near(0, n)
+    for n in range(CUTS):
+        part0(0, n, 1 - y).wait_send()
     for slot in range(4):
         for q in range(PIECES):
             nxt_load(slot, q).wait()
@@ -361,66 +421,69 @@
     def _(k):
         near_layer1(k)
 
-        @pl.when(k < OWN - 1)
-        def _():
-            near(k + 1)
-
         @pl.when(k == OWN - 1)
         def _():
-            for early in range(OWN - 2):
-                far_x(early)
+            pass_x_all(0)
 
         @pl.when(k >= 1)
         def _():
             far(k - 1)
 
-    far_x(OWN - 2)
-    far(OWN - 1)
-    far_x(OWN - 1)
-
-    lag = 2
-
-    @pl.loop(0, OWN * HALVES + lag)
+    far(OWN - 1, lambda: pass_x_all(1))
+
+    for copy in biases:
+        copy.wait_send()
+    for q in range(PIECES):
+        for copies in (own_core, own_x, nxt_core, nxt_y, fwd_y):
+            copies[q].wait_send()
+    for k in range(OWN):
+        part1(k, 1 - x).wait_send()
+        for n in range(CUTS):
+            if k > 0:
+                part0(k, n, 1 - y).wait_send()
+
+    early, lag, last = 2, 6, 8
+    total = OWN * PARTS
+
+    @pl.loop(0, total + last)
     def _(j):
-        @pl.when(j < OWN * HALVES)
-        def _():
-            k, n = j // HALVES, j % HALVES
-            by_x, by_y, *_ = come(k, n)
-            to_d, x_core, y_core, _ = pass_on(k, n)
-            by_y.wait_recv()
-            y_core.start()
-            by_x.wait_recv()
-            to_d.start()
-            x_core.start()
-
-        @pl.when(j >= lag)
-        def _():
-            k, n = (j - lag) // HALVES, (j - lag) % HALVES
+        @pl.when(j < total)
+        def _():
+            k, n = j // PARTS, j % PARTS
+            come(k, n)[1].wait_recv()
+
+            @pl.when(j >= TURN)
+            def _():
+                pass_on(k, n)[1].start()
+
+            @pl.when(n == PARTS - 1)
+            def _():
+                pass_y(k).start()
+
+        @pl.when((j >= early * PARTS) & (j < total))
+        def _():
+            pass_x(j // PARTS, j % PARTS)
+
+        @pl.when((j >= lag) & (j < total + lag))
+        def _():
+            k, n = (j - lag) // PARTS, (j - lag) % PARTS
             come(k, n)[2].wait_recv()
             pass_on(k, n)[3].start()
 
-    @pl.loop(0, OWN)
-    def _(k):
-        part1(k).wait_send()
-        for n in range(CUTS):
-            part0(k, n).wait_send()
-            give0(k, n).wait_send()
-        for n in range(HALVES):
-            local, *others = put(k, n)
-            local.wait()
-            for copy in (*others, *pass_on(k, n)):
+        @pl.when(j >= last)
+        def _():
+            k, n = (j - last) // PARTS, (j - last) % PARTS
+            for copy in (*put(k, n), *pass_on(k, n)[1:]):
                 copy.wait_send()
             for copy in come(k, n)[3:]:
                 copy.wait_recv()
 
-    for copy in biases:
-        copy.wait_send()
-    for q in range(PIECES):
-        own_core[q].wait_send()
-        own_x[q].wait_send()
-        nxt_core[q].wait_send()
-        nxt_y[q].wait_send()
-        fwd_y[q].wait_send()
+            @pl.when(n == PARTS - 1)
+            def _():
+                for copy in (put_core(k), pass_y(k)):
+                    copy.wait_send()
+                for copy in come_core(k):
+                    copy.wait_recv()
 
 
 def solution(mesh):
@@ -440,14 +503,14 @@
         encoded, *_ = pl.pallas_call(
             fused,
             out_shape=(
-                shape((n_images * seq, dim), BF16),
+                pltpu.VMEM((n_images * seq, dim), BF16),
                 shape((3, 3 * heads_w, dim), BF16),
                 shape((3, heads_w, dim), BF16),
                 shape((3, dim, mlp), BF16),
                 shape((3, mlp, dim), BF16),
             ),
             in_specs=[any_spec] * 7 + [vm_spec] * 6,
-            out_specs=(any_spec,) * 5,
+            out_specs=(vm_spec,) + (any_spec,) * 4,
             scratch_shapes=[
                 pltpu.VMEM((4, 3 * heads_w, dim), BF16),
                 pltpu.VMEM((4, heads_w, dim), BF16),
@@ -457,15 +520,15 @@
                 pltpu.VMEM((layers, 2, q_scale.shape[1], seq), F32),
                 pltpu.VMEM((IMGS, seq, dim), F32),
                 pltpu.VMEM((IMGS, seq, dim), BF16),
-                pltpu.VMEM((IMGS, seq, dim), BF16),
-                *[pltpu.VMEM((OWN, seq, dim), BF16)] * 5,
+                pltpu.VMEM((OWN, seq, dim), BF16),
                 dma(PIECES), dma(4, PIECES), dma(IMGS), dma(5), dma(5),
                 *[dma(PIECES)] * 12,
                 *[dma(OWN, CUTS)] * 4, dma(OWN), dma(OWN),
-                *[dma(OWN, HALVES)] * 15,
+                *[dma(OWN)] * 4,
+                *[dma(OWN, PARTS)] * 10,
             ],
             compiler_params=pltpu.CompilerParams(
-                collective_id=0, has_side_effects=True, vmem_limit_bytes=67000000),
+                collective_id=0, has_side_effects=True, vmem_limit_bytes=45500000),
         )(tokens_in.reshape(n_images * seq, dim), across(w_query), across(w_key), across(w_value), w_out, w_up, w_down, ln_scale, q_scale, k_scale, b_out, b_up, b_down)
         return encoded.reshape(n_images, seq, dim)
 

time: 337 us -> 317 us (0.941)
  Pallas kernels: 319 us -> 309 us
  local copies, waits for them, and re-layouts: 17.4 us -> 7.54 us
    pallas_call x1, Pallas kernels: 319 us -> 309 us  [per_device(): pl.pallas_call(fused, out_shape=(pltpu.VMEM((n_images * seq, dim), BF16),...]
    unnamed x1, local copies, waits for them, and re-layouts: 17.4 us -> 7.54 us
where the time goes in v3:
time: 317 us
  Pallas kernels  309 us (97%)
  local copies, waits for them, and re-layouts  7.54 us (2%)
    pallas_call x1, Pallas kernels, per_device(): pl.pallas_call(fused, out_shape=(pltpu.VMEM((n_images * seq, dim), BF16),...  309 us
    unnamed x1, local copies, waits for them, and re-layouts  7.54 us

profile of v3, /device:TPU:0, one launch (start us, length us, event | category | flops | bytes accessed | tf_op | source)
XLA Modules:
  0.0 316.8 jit_solution(3872740123576523438)
XLA Ops:
  0.0 309.2 %shard_map.127 = (bf16[8192,1280]{1,0:T(8,128)(2,1)S(1)}, bf16[3,480,1280]{2,1,0:T(8,128)(2,1)}, bf16[3,160,1280]{2,1,0:T(8,128)(2,1)}, bf16[3,1280,640]{2,1,0:T(8,128)(2,1)}, bf16[3,640,1280]{2,1,0:T(8,128)(2,1)}) custom-call(bf16[8192,1280]{1,0:T(8,128)(2,1)} %bitcast.6, bf16[2,160,1280]{2,1,0:T(8,128)(2,1)} %bitcast.7, bf16[2,160,1280]{2,1,0:T(8,128)(2,1)} %bitcast.8, ...), custom_call_target="tpu_custom_call" | custom-call | tf_op jit(solution)/shard_map/pallas_call | solution.py:503
  309.2 7.5 %copy.15 = bf16[32,256,1280]{2,1,0:T(8,128)(2,1)} copy(bf16[32,256,1280]{2,1,0:T(8,128)(2,1)S(1)} %bitcast.5) | data formatting | bytes 41943040

commit v4 on v3

--- a/solution.py
+++ b/solution.py
@@ -14,7 +14,7 @@
 SPLIT = 384
 PIECES = 8
 CUTS = 4
-PARTS = 4
+PARTS = CUTS
 TURN = 14
 
 
@@ -35,9 +35,9 @@
 
 
 def fused(
-    tok, wq, wk, wv, wo, w1, w2, ln, qs, ks, bo, bu, b2,
+    tok, wq, wk, wv, wo, w1, w2, bu, ln_in, qs_in, ks_in, bo_in, b2_in,
     out, gq, go, g1, g2,
-    vq, vo, v1, v2, vb, gain, acc, hid, x1,
+    vq, vo, v1, v2, vb, ln, qs, ks, bo, b2, gain, acc, hid, x1, s_v,
     loc0, loc1, xs, s_b, r_b,
     s_c0, r_c0, s_x0, r_x0, s_f0, r_f0,
     s_c1, r_c1, s_y1, r_y1, s_f1, r_f1,
@@ -65,6 +65,16 @@
             src_ref=src, dst_ref=dst, send_sem=send, recv_sem=recv,
             device_id={"tp": dev}, device_id_type=MESH)
 
+    def all_of(sem, rows):
+        ref = out.at[pl.ds(0, rows), :]
+        return pltpu.make_async_copy(ref, ref, sem)
+
+    def filled(sem, rows):
+        all_of(sem, rows).wait()
+
+    sent = filled
+    BLOCK = 3 * heads_w + heads_w + 2 * mlp
+
     def pieces_of(layer):
         return (
             wq.at[layer], wk.at[layer], wv.at[layer], wo.at[layer],
@@ -85,9 +95,9 @@
     land = (gq, go, g1, g2)
 
     def moves(src, dst, send, recv, dev):
-        return [remote(src[q], dst[q], send.at[q], recv.at[q], dev) for q in range(PIECES)]
-
-    own_load = [pltpu.make_async_copy(pieces_of(0)[q], slot_of(vmem, 0)[q], loc0.at[q]) for q in range(PIECES)]
+        return [remote(src[q], dst[q], send, recv.at[q], dev) for q in range(PIECES)]
+
+    own_load = [pltpu.make_async_copy(pieces_of(0)[q], slot_of(vmem, 0)[q], loc0) for q in range(PIECES)]
     own_core = moves(pieces_of(0), slot_of(vmem, 1), s_c0, r_c0, cp)
     own_x = moves(pieces_of(0), slot_of(vmem, 2), s_x0, r_x0, xp)
     fwd_x = moves(slot_of(vmem, 2), slot_of(vmem, 3), s_f0, r_f0, cp)
@@ -99,7 +109,7 @@
 
     def nxt_load(slot, q):
         src = pieces_of(1) if slot == 0 else slot_of(land, slot - 1)
-        return pltpu.make_async_copy(src[q], slot_of(vmem, slot)[q], loc1.at[slot, q])
+        return pltpu.make_async_copy(src[q], slot_of(vmem, slot)[q], loc1.at[slot])
 
     group = (2 * x + c) * IMGS
 
@@ -113,10 +123,17 @@
     barrier = pltpu.get_barrier_semaphore()
     for dev in peers:
         pl.semaphore_signal(barrier, inc=1, device_id={"tp": dev}, device_id_type=MESH)
-    for q in range(PIECES):
-        own_load[q].start()
+    small = [
+        pltpu.make_async_copy(src, dst, s_v.at[n])
+        for n, (src, dst) in enumerate(
+            ((ln_in, ln), (qs_in, qs), (ks_in, ks), (bo_in, bo), (b2_in, b2), (bu, vb.at[0])))
+    ]
+    for copy in small:
+        copy.start()
     for i in range(IMGS):
         load_x(i).start()
+    for q in range(PIECES):
+        own_load[q].start()
     pl.semaphore_wait(barrier, len(peers))
 
     for copy in biases:
@@ -131,7 +148,8 @@
     def row(ref, layer):
         return ref[layer : layer + 1, :].astype(F32)
 
-    vb[0] = bu[...]
+    for copy in small:
+        copy.wait()
     for layer in range(2):
         for n, ref in enumerate((qs, ks)):
             gain[layer, n] = jnp.broadcast_to(row(ref, layer), (seq, head_dim)).T
@@ -142,26 +160,59 @@
         variance = jnp.mean(centered * centered, axis=0, keepdims=True)
         return centered * lax.rsqrt(variance + LN_EPS) * gain[layer, n]
 
+    def heads_of(i, slot):
+        return lax.dot_general(vq[slot], hid[i], (((1,), (1,)), ((), ())), preferred_element_type=F32)
+
+    def head_inputs(proj, hd, layer):
+        lo = hd * head_dim
+        q_h = head_norm(proj[lo : lo + head_dim], layer, 0).astype(BF16)
+        k_h = head_norm(proj[heads_w + lo : heads_w + lo + head_dim], layer, 1).astype(BF16).T
+        v_h = proj[2 * heads_w + lo : 2 * heads_w + lo + head_dim].astype(BF16)
+        return q_h, k_h, v_h
+
+    def softmax(scores):
+        scores = scores * head_dim ** -0.5
+        weight = jnp.exp(scores - jnp.max(scores, axis=0, keepdims=True))
+        total = jnp.sum(weight, axis=0, keepdims=True)
+        return (weight * (1.0 / total)).astype(BF16)
+
     def attend(i, slot, layer):
-        proj = lax.dot_general(vq[slot], hid[i], (((1,), (1,)), ((), ())), preferred_element_type=F32)
-        mixed = []
-        for hd in range(n_heads):
-            lo = hd * head_dim
-            q_h = head_norm(proj[lo : lo + head_dim], layer, 0).astype(BF16)
-            k_h = head_norm(proj[heads_w + lo : heads_w + lo + head_dim], layer, 1).T.astype(BF16)
-            v_h = proj[2 * heads_w + lo : 2 * heads_w + lo + head_dim].astype(BF16)
-            scores = dot(k_h, q_h) * head_dim ** -0.5
-            weight = jnp.exp(scores - jnp.max(scores, axis=0, keepdims=True))
-            total = jnp.sum(weight, axis=0, keepdims=True)
-            prob = (weight * (1.0 / total)).astype(BF16)
-            mixed.append(dot(v_h, prob))
-        mix = jnp.concatenate(mixed, axis=0).T.astype(BF16)
+        proj = heads_of(i, slot)
+        parts = [head_inputs(proj, hd, layer) for hd in range(n_heads)]
+        scores = [dot(k_h, q_h) for q_h, k_h, _ in parts]
+        mixed = [dot(v_h, softmax(sc)) for (_, _, v_h), sc in zip(parts, scores)]
+        mix = jnp.concatenate(mixed, axis=0).astype(BF16).T
         return dot(mix, vo[slot])
 
     def mlp_part(i, slot, layer, lo, hi):
         bias = vb[slot + 2 * layer * (slot // 2), layer : layer + 1, lo:hi].astype(F32)
         act = gelu(dot(hid[i], v1[slot, :, lo:hi]) + bias).astype(BF16)
         return dot(act, v2[slot, lo:hi, :])
+
+    def both(i, slot, layer):
+        proj = heads_of(i, slot)
+        row_b = vb[slot + 2 * layer * (slot // 2), layer : layer + 1, :].astype(F32)
+        bounds = (0, 256, 512, 640)
+
+        def up(n):
+            lo, hi = bounds[n], bounds[n + 1]
+            return dot(hid[i], v1[slot, :, lo:hi]) + row_b[:, lo:hi]
+
+        def down(n, pre):
+            return dot(gelu(pre).astype(BF16), v2[slot, bounds[n] : bounds[n + 1], :])
+
+        pre0 = up(0)
+        parts = [head_inputs(proj, hd, layer) for hd in range(n_heads)]
+        pre1 = up(1)
+        scores = [dot(k_h, q_h) for q_h, k_h, _ in parts]
+        pre2 = up(2)
+        sum0 = down(0, pre0)
+        probs = [softmax(sc) for sc in scores]
+        sum1 = down(1, pre1)
+        mixed = [dot(v_h, prob) for (_, _, v_h), prob in zip(parts, probs)]
+        sum2 = down(2, pre2)
+        mix = jnp.concatenate(mixed, axis=0).astype(BF16).T
+        return sum0 + sum1 + sum2 + dot(mix, vo[slot])
 
     @pl.loop(0, IMGS)
     def _(i):
@@ -181,8 +232,7 @@
     def _(slot):
         @pl.when(slot == 0)
         def _():
-            for q in range(PIECES):
-                own_load[q].wait()
+            filled(loc0, BLOCK)
             for copy in biases:
                 copy.wait_recv()
 
@@ -193,7 +243,7 @@
 
         @pl.loop(0, IMGS)
         def _(i):
-            acc[i] += attend(i, slot, 0) + mlp_part(i, slot, 0, 0, mlp)
+            acc[i] += both(i, slot, 0)
 
     for q in range(PIECES):
         nxt_core[q].wait_recv()
@@ -253,29 +303,45 @@
         return pl.ds(pl.multiple_of(rows_of(1 - x, chip_y, c, k) + n * (seq // CUTS), seq // CUTS), seq // CUTS)
 
     def part0(k, n, chip_y):
-        return remote(hid.at[k, cut(n), :], out.at[lent(chip_y, k, n), :], s_p0.at[k, n], r_p0.at[k, n], yp)
+        return remote(hid.at[k, cut(n), :], out.at[lent(chip_y, k, n), :], s_p0.at[k], r_p0.at[k, n], yp)
 
     def give0(k, n):
-        return remote(out.at[lent(y, k, n), :], x1.at[k, cut(n), :], s_g0.at[k, n], r_g0.at[k, n], xp)
-
-    def part1(k, chip_x):
-        return remote(hid.at[OWN + k], out.at[pl.ds(rows_of(chip_x, y, c, k), seq), :], s_p1.at[k], r_p1.at[k], xp)
-
-    @pl.loop(0, IMGS)
-    def _(i):
-        acc[i] += mlp_part(i, 2, 0, SPLIT, mlp) + mlp_part(i, 3, 0, SPLIT, mlp)
-
-        @pl.when(i < OWN)
-        def _():
-            hid[i] = acc[i].astype(BF16)
-            for n in range(CUTS):
-                part0(i, n, 1 - y).start()
-
-    for q in (6, 7):
-        nxt_y[q].wait_recv()
-        fwd_y[q].start()
-    for q in range(PIECES):
-        fwd_x[q].wait_send()
+        return remote(out.at[lent(y, k, n), :], x1.at[k, cut(n), :], s_g0.at[k], r_g0.at[k, n], xp)
+
+    def part1(k, n, chip_x):
+        rows = pl.ds(pl.multiple_of(rows_of(chip_x, y, c, k) + n * (seq // CUTS), seq // CUTS), seq // CUTS)
+        return remote(hid.at[OWN + k, cut(n), :], out.at[rows, :], s_p1, r_p1.at[k, n], xp)
+
+    def near(k, n):
+        part0(k, n, y).wait_recv()
+        rows = lent(y, k, n)
+        out[rows, :] = (acc[OWN + k, cut(n), :] + out[rows, :].astype(F32)).astype(BF16)
+        give0(k, n).start()
+
+    @pl.loop(0, OWN)
+    def _(k):
+        @pl.loop(0, 2)
+        def _(mine):
+            i = k + OWN * mine
+            acc[i] += mlp_part(i, 2, 0, SPLIT, mlp) + mlp_part(i, 3, 0, SPLIT, mlp)
+
+            @pl.when(mine == 0)
+            def _():
+                hid[k] = acc[k].astype(BF16)
+                for n in range(CUTS):
+                    part0(k, n, 1 - y).start()
+
+        @pl.when(k == 0)
+        def _():
+            for q in (6, 7):
+                nxt_y[q].wait_recv()
+                fwd_y[q].start()
+
+        @pl.when(k >= 1)
+        def _():
+            near(0, k - 1)
+
+    sent(s_f0, BLOCK)
     for q in range(PIECES):
         nxt_load(2, q).start()
     for q in range(PIECES):
@@ -293,7 +359,7 @@
 
         @pl.loop(0, 4)
         def _(slot):
-            acc[0] += attend(0, slot, 1) + mlp_part(0, slot, 1, 0, mlp)
+            acc[0] += both(0, slot, 1)
             if between is not None:
                 between(slot)
 
@@ -305,24 +371,17 @@
 
     def put_core(k):
         ref = image_at(x, y, c, k)
-        return remote(ref, ref, s_oc.at[k], r_oc.at[k], cp)
+        return remote(ref, ref, s_oc, r_oc, cp)
 
     def pass_y(k):
         ref = image_at(x, 1 - y, c, k)
-        return remote(ref, ref, s_ey.at[k], r_ey.at[k], cp)
-
-    def come_core(k):
-        own, of_y = image_at(x, y, 1 - c, k), image_at(x, 1 - y, 1 - c, k)
-        return (
-            remote(own, own, s_oc.at[k], r_oc.at[k], cp),
-            remote(of_y, of_y, s_ey.at[k], r_ey.at[k], cp),
-        )
+        return remote(ref, ref, s_ey, r_ey, cp)
 
     def put(k, n):
         ref = part_of(x, y, c, k, n)
         return (
-            remote(ref, ref, s_oy.at[k, n], r_oy.at[k, n], yp),
-            remote(ref, ref, s_ox.at[k, n], r_ox.at[k, n], xp),
+            remote(ref, ref, s_oy, r_oy.at[k, n], yp),
+            remote(ref, ref, s_ox, r_ox.at[k, n], xp),
         )
 
     def pass_on(k, n):
@@ -330,29 +389,21 @@
         of_y = part_of(x, 1 - y, c, k, n)
         of_d = part_of(1 - x, 1 - y, c, k, n)
         return (
-            remote(of_x, of_x, s_od.at[k, n], r_od.at[k, n], yp),
-            remote(of_y, of_y, s_od.at[k, n], r_od.at[k, n], xp),
-            remote(of_x, of_x, s_ex.at[k, n], r_ex.at[k, n], cp),
-            remote(of_d, of_d, s_ed.at[k, n], r_ed.at[k, n], cp),
+            remote(of_x, of_x, s_od, r_od.at[k, n], yp),
+            remote(of_y, of_y, s_od, r_od.at[k, n], xp),
+            remote(of_x, of_x, s_ex, r_ex, cp),
+            remote(of_d, of_d, s_ed, r_ed, cp),
         )
 
     def come(k, n):
         def into(ref, recv):
-            return remote(ref, ref, s_ox.at[k, n], recv.at[k, n], cp)
+            return remote(ref, ref, s_ox, recv.at[k, n], cp)
 
         return (
             into(part_of(1 - x, y, c, k, n), r_ox),
             into(part_of(x, 1 - y, c, k, n), r_oy),
             into(part_of(1 - x, 1 - y, c, k, n), r_od),
-            into(part_of(1 - x, y, 1 - c, k, n), r_ex),
-            into(part_of(1 - x, 1 - y, 1 - c, k, n), r_ed),
         )
-
-    def near(k, n):
-        part0(k, n, y).wait_recv()
-        rows = lent(y, k, n)
-        out[rows, :] = (acc[OWN + k, cut(n), :] + out[rows, :].astype(F32)).astype(BF16)
-        give0(k, n).start()
 
     def near_behind(k, when):
         def between(slot):
@@ -372,10 +423,10 @@
         rows = pl.ds(pl.multiple_of(rows_of(1 - x, y, c, k), seq), seq)
         layer1(out[rows, :], False, between)
         hid[OWN + k] = acc[0].astype(BF16)
+        rest()
+        sent(s_g0.at[k], seq)
         for n in range(CUTS):
-            give0(k, n).wait_send()
-        part1(k, 1 - x).start()
-        rest()
+            part1(k, n, 1 - x).start()
 
     def far(k, before=None):
         for n in range(CUTS):
@@ -387,13 +438,14 @@
         else:
             layer1(x1[k], True)
             before()
-        part1(k, x).wait_recv()
-        rows = pl.ds(pl.multiple_of(rows_of(x, y, c, k), seq), seq)
-        out[rows, :] = (acc[0] + out[rows, :].astype(F32)).astype(BF16)
-        put_core(k).start()
-        for n in range(PARTS):
+        first = rows_of(x, y, c, k)
+        for n in range(CUTS):
+            part1(k, n, x).wait_recv()
+            rows = pl.ds(pl.multiple_of(first + n * (seq // CUTS), seq // CUTS), seq // CUTS)
+            out[rows, :] = (acc[0, cut(n), :] + out[rows, :].astype(F32)).astype(BF16)
             for copy in put(k, n):
                 copy.start()
+        put_core(k).start()
 
     def pass_x(k, n):
         come(k, n)[0].wait_recv()
@@ -409,13 +461,10 @@
         for n in range(PARTS):
             pass_x(k, n)
 
-    for n in range(CUTS):
-        near(0, n)
-    for n in range(CUTS):
-        part0(0, n, 1 - y).wait_send()
+    near(0, CUTS - 1)
+    sent(s_p0.at[0], seq)
     for slot in range(4):
-        for q in range(PIECES):
-            nxt_load(slot, q).wait()
+        filled(loc1.at[slot], BLOCK)
 
     @pl.loop(0, OWN)
     def _(k):
@@ -433,19 +482,16 @@
 
     for copy in biases:
         copy.wait_send()
-    for q in range(PIECES):
-        for copies in (own_core, own_x, nxt_core, nxt_y, fwd_y):
-            copies[q].wait_send()
-    for k in range(OWN):
-        part1(k, 1 - x).wait_send()
-        for n in range(CUTS):
-            if k > 0:
-                part0(k, n, 1 - y).wait_send()
-
-    early, lag, last = 2, 6, 8
+    for sem in (s_c0, s_x0, s_c1, s_y1, s_f1):
+        sent(sem, BLOCK)
+    for k in range(1, OWN):
+        sent(s_p0.at[k], seq)
+    sent(s_p1, OWN * seq)
+
+    early, lag = 2, 6
     total = OWN * PARTS
 
-    @pl.loop(0, total + last)
+    @pl.loop(0, total + lag)
     def _(j):
         @pl.when(j < total)
         def _():
@@ -464,26 +510,14 @@
         def _():
             pass_x(j // PARTS, j % PARTS)
 
-        @pl.when((j >= lag) & (j < total + lag))
+        @pl.when(j >= lag)
         def _():
             k, n = (j - lag) // PARTS, (j - lag) % PARTS
             come(k, n)[2].wait_recv()
             pass_on(k, n)[3].start()
 
-        @pl.when(j >= last)
-        def _():
-            k, n = (j - last) // PARTS, (j - last) % PARTS
-            for copy in (*put(k, n), *pass_on(k, n)[1:]):
-                copy.wait_send()
-            for copy in come(k, n)[3:]:
-                copy.wait_recv()
-
-            @pl.when(n == PARTS - 1)
-            def _():
-                for copy in (put_core(k), pass_y(k)):
-                    copy.wait_send()
-                for copy in come_core(k):
-                    copy.wait_recv()
+    for sem in (s_oc, s_ey, s_ox, s_oy, s_od, s_ex, s_ed, r_oc, r_ey, r_ex, r_ed):
+        sent(sem, OWN * seq)
 
 
 def solution(mesh):
@@ -499,6 +533,7 @@
         any_spec = pl.BlockSpec(memory_space=pl.ANY)
         vm_spec = pl.BlockSpec(memory_space=pltpu.VMEM)
         dma = lambda *shape: pltpu.SemaphoreType.DMA(shape)
+        one = pltpu.SemaphoreType.DMA
         shape = jax.ShapeDtypeStruct
         encoded, *_ = pl.pallas_call(
             fused,
@@ -509,7 +544,7 @@
                 shape((3, dim, mlp), BF16),
                 shape((3, mlp, dim), BF16),
             ),
-            in_specs=[any_spec] * 7 + [vm_spec] * 6,
+            in_specs=[any_spec] * 13,
             out_specs=(vm_spec,) + (any_spec,) * 4,
             scratch_shapes=[
                 pltpu.VMEM((4, 3 * heads_w, dim), BF16),
@@ -517,19 +552,22 @@
                 pltpu.VMEM((4, dim, mlp), BF16),
                 pltpu.VMEM((4, mlp, dim), BF16),
                 pltpu.VMEM((6, layers, mlp), BF16),
+                *[pltpu.VMEM(v.shape, BF16) for v in (ln_scale, q_scale, k_scale, b_out, b_down)],
                 pltpu.VMEM((layers, 2, q_scale.shape[1], seq), F32),
                 pltpu.VMEM((IMGS, seq, dim), F32),
                 pltpu.VMEM((IMGS, seq, dim), BF16),
                 pltpu.VMEM((OWN, seq, dim), BF16),
-                dma(PIECES), dma(4, PIECES), dma(IMGS), dma(5), dma(5),
-                *[dma(PIECES)] * 12,
-                *[dma(OWN, CUTS)] * 4, dma(OWN), dma(OWN),
-                *[dma(OWN)] * 4,
-                *[dma(OWN, PARTS)] * 10,
+                dma(6),
+                one, dma(4), dma(IMGS), dma(5), dma(5),
+                *[one, dma(PIECES)] * 6,
+                *[dma(OWN), dma(OWN, CUTS)] * 2, one, dma(OWN, CUTS),
+                *[one] * 4,
+                *[one, dma(OWN, PARTS)] * 3,
+                *[one] * 4,
             ],
             compiler_params=pltpu.CompilerParams(
                 collective_id=0, has_side_effects=True, vmem_limit_bytes=45500000),
-        )(tokens_in.reshape(n_images * seq, dim), across(w_query), across(w_key), across(w_value), w_out, w_up, w_down, ln_scale, q_scale, k_scale, b_out, b_up, b_down)
+        )(tokens_in.reshape(n_images * seq, dim), across(w_query), across(w_key), across(w_value), w_out, w_up, w_down, b_up, ln_scale, q_scale, k_scale, b_out, b_down)
         return encoded.reshape(n_images, seq, dim)
 
     return jax.shard_map(per_device, mesh=mesh, in_specs=in_specs, out_specs=P("dp", None, None), check_vma=False)

time: 317 us -> 310 us (0.978)
  Pallas kernels: 309 us -> 302 us
    pallas_call x1, Pallas kernels: 309 us -> 302 us  [per_device(): pl.pallas_call(fused, out_shape=(pltpu.VMEM((n_images * seq, dim), BF16),...]
where the time goes in v4:
time: 310 us; the launch traced here: 309 us
  Pallas kernels  302 us (97%)
  local copies, waits for them, and re-layouts  7.54 us (2%)
    pallas_call x1, Pallas kernels, per_device(): pl.pallas_call(fused, out_shape=(pltpu.VMEM((n_images * seq, dim), BF16),...  302 us
    unnamed x1, local copies, waits for them, and re-layouts  7.54 us

profile of v4, /device:TPU:0, one launch (start us, length us, event | category | flops | bytes accessed | tf_op | source)
XLA Modules:
  0.0 309.4 jit_solution(8090406971377159059)
XLA Ops:
  0.0 301.9 %shard_map.127 = (bf16[8192,1280]{1,0:T(8,128)(2,1)S(1)}, bf16[3,480,1280]{2,1,0:T(8,128)(2,1)}, bf16[3,160,1280]{2,1,0:T(8,128)(2,1)}, bf16[3,1280,640]{2,1,0:T(8,128)(2,1)}, bf16[3,640,1280]{2,1,0:T(8,128)(2,1)}) custom-call(bf16[8192,1280]{1,0:T(8,128)(2,1)} %bitcast.6, bf16[2,160,1280]{2,1,0:T(8,128)(2,1)} %bitcast.7, bf16[2,160,1280]{2,1,0:T(8,128)(2,1)} %bitcast.8, ...), custom_call_target="tpu_custom_call" | custom-call | tf_op jit(solution)/shard_map/pallas_call | solution.py:538
  301.9 7.5 %copy.15 = bf16[32,256,1280]{2,1,0:T(8,128)(2,1)} copy(bf16[32,256,1280]{2,1,0:T(8,128)(2,1)S(1)} %bitcast.5) | data formatting | bytes 41943040

commit v5 on v4

--- a/solution.py
+++ b/solution.py
@@ -15,7 +15,7 @@
 PIECES = 8
 CUTS = 4
 PARTS = CUTS
-TURN = 14
+TURN = 15
 
 
 def normalize(values):
@@ -349,20 +349,6 @@
     for q in range(PIECES):
         nxt_load(3, q).start()
 
-    def layer1(values, finish, between=None):
-        values = values.astype(F32)
-        hid[0] = (normalize(values) * row(ln, 1)).astype(BF16)
-        if finish:
-            acc[0] = values + row(bo, 1) + row(b2, 1)
-        else:
-            acc[0] = jnp.zeros((seq, dim), F32)
-
-        @pl.loop(0, 4)
-        def _(slot):
-            acc[0] += both(0, slot, 1)
-            if between is not None:
-                between(slot)
-
     def part_of(chip_x, chip_y, core, k, n):
         return out.at[pl.ds(rows_of(chip_x, chip_y, core, k) + n * (seq // PARTS), seq // PARTS), :]
 
@@ -405,44 +391,16 @@
             into(part_of(1 - x, 1 - y, c, k, n), r_od),
         )
 
-    def near_behind(k, when):
-        def between(slot):
-            @pl.when(when & (slot >= 1))
-            def _():
-                near(k, slot - 1)
-
-        def rest():
-            @pl.when(when)
-            def _():
-                near(k, CUTS - 1)
-
-        return between, rest
-
-    def near_layer1(k):
-        between, rest = near_behind(k + 1, k < OWN - 2)
-        rows = pl.ds(pl.multiple_of(rows_of(1 - x, y, c, k), seq), seq)
-        layer1(out[rows, :], False, between)
-        hid[OWN + k] = acc[0].astype(BF16)
-        rest()
+    def start_part1(k):
         sent(s_g0.at[k], seq)
         for n in range(CUTS):
             part1(k, n, 1 - x).start()
 
-    def far(k, before=None):
-        for n in range(CUTS):
-            give0(k, n).wait_recv()
-        if before is None:
-            between, rest = near_behind(OWN - 1, k == 0)
-            layer1(x1[k], True, between)
-            rest()
-        else:
-            layer1(x1[k], True)
-            before()
-        first = rows_of(x, y, c, k)
+    def finish(k):
         for n in range(CUTS):
             part1(k, n, x).wait_recv()
-            rows = pl.ds(pl.multiple_of(first + n * (seq // CUTS), seq // CUTS), seq // CUTS)
-            out[rows, :] = (acc[0, cut(n), :] + out[rows, :].astype(F32)).astype(BF16)
+            rows = pl.ds(pl.multiple_of(rows_of(x, y, c, k) + n * (seq // CUTS), seq // CUTS), seq // CUTS)
+            out[rows, :] = (acc[k, cut(n), :] + out[rows, :].astype(F32)).astype(BF16)
             for copy in put(k, n):
                 copy.start()
         put_core(k).start()
@@ -466,19 +424,73 @@
     for slot in range(4):
         filled(loc1.at[slot], BLOCK)
 
-    @pl.loop(0, OWN)
-    def _(k):
-        near_layer1(k)
-
-        @pl.when(k == OWN - 1)
+    @pl.loop(0, 2 * OWN)
+    def _(t):
+        theirs = (t == 2) | (t == 4) | (t >= 6)
+        k_own, k_their = (t + 1) // 2, (t - 1) // 2
+
+        @pl.when(jnp.logical_not(theirs))
+        def _():
+            values = out[pl.ds(pl.multiple_of(rows_of(1 - x, y, c, k_own), seq), seq), :].astype(F32)
+            hid[0] = (normalize(values) * row(ln, 1)).astype(BF16)
+            acc[0] = jnp.zeros((seq, dim), F32)
+
+        @pl.when(theirs)
+        def _():
+            for n in range(CUTS):
+                give0(k_their, n).wait_recv()
+            values = x1[k_their].astype(F32)
+            hid[0] = (normalize(values) * row(ln, 1)).astype(BF16)
+            acc[k_their] = values + row(bo, 1) + row(b2, 1)
+
+        where = jnp.where(theirs, k_their, 0)
+
+        @pl.loop(0, 4)
+        def _(slot):
+            acc[where] += both(0, slot, 1)
+
+            @pl.when((t <= 1) & (slot != 1))
+            def _():
+                near(t + 1, slot // 2 + slot // 3)
+
+            @pl.when((t == 7) & (slot >= 2))
+            def _():
+                pass_x(1, slot - 2)
+
+        @pl.when(jnp.logical_not(theirs))
+        def _():
+            hid[OWN + k_own] = acc[0].astype(BF16)
+
+        @pl.when(t <= 1)
+        def _():
+            near(t + 1, CUTS - 1)
+            start_part1(t)
+
+        @pl.when((t == 2) | (t == 4))
+        def _():
+            finish(k_their)
+
+        @pl.when(t == 2)
+        def _():
+            for n in range(CUTS):
+                near(OWN - 1, n)
+
+        @pl.when(t == 4)
+        def _():
+            start_part1(2)
+
+        @pl.when(t == 5)
         def _():
             pass_x_all(0)
 
-        @pl.when(k >= 1)
-        def _():
-            far(k - 1)
-
-    far(OWN - 1, lambda: pass_x_all(1))
+        @pl.when(t == 6)
+        def _():
+            start_part1(3)
+
+    for n in range(2, PARTS):
+        pass_x(1, n)
+    finish(2)
+    finish(3)
 
     for copy in biases:
         copy.wait_send()

time: 310 us -> 307 us (level)
  no operation moved by 1% of the time
where the time goes in v5:
time: 307 us; the launch traced here: 306 us
  Pallas kernels  299 us (97%)
  local copies, waits for them, and re-layouts  7.54 us (2%)
    pallas_call x1, Pallas kernels, per_device(): pl.pallas_call(fused, out_shape=(pltpu.VMEM((n_images * seq, dim), BF16),...  299 us
    unnamed x1, local copies, waits for them, and re-layouts  7.54 us

profile of v5, /device:TPU:0, one launch (start us, length us, event | category | flops | bytes accessed | tf_op | source)
XLA Modules:
  0.0 306.5 jit_solution(15878134987284742811)
XLA Ops:
  0.0 298.9 %shard_map.127 = (bf16[8192,1280]{1,0:T(8,128)(2,1)S(1)}, bf16[3,480,1280]{2,1,0:T(8,128)(2,1)}, bf16[3,160,1280]{2,1,0:T(8,128)(2,1)}, bf16[3,1280,640]{2,1,0:T(8,128)(2,1)}, bf16[3,640,1280]{2,1,0:T(8,128)(2,1)}) custom-call(bf16[8192,1280]{1,0:T(8,128)(2,1)} %bitcast.6, bf16[2,160,1280]{2,1,0:T(8,128)(2,1)} %bitcast.7, bf16[2,160,1280]{2,1,0:T(8,128)(2,1)} %bitcast.8, ...), custom_call_target="tpu_custom_call" | custom-call | tf_op jit(solution)/shard_map/pallas_call | solution.py:550
  298.9 7.5 %copy.15 = bf16[32,256,1280]{2,1,0:T(8,128)(2,1)} copy(bf16[32,256,1280]{2,1,0:T(8,128)(2,1)S(1)} %bitcast.5) | data formatting | bytes 41943040

commit v6 on v5

--- a/solution.py
+++ b/solution.py
@@ -396,13 +396,16 @@
         for n in range(CUTS):
             part1(k, n, 1 - x).start()
 
-    def finish(k):
-        for n in range(CUTS):
-            part1(k, n, x).wait_recv()
-            rows = pl.ds(pl.multiple_of(rows_of(x, y, c, k) + n * (seq // CUTS), seq // CUTS), seq // CUTS)
-            out[rows, :] = (acc[k, cut(n), :] + out[rows, :].astype(F32)).astype(BF16)
-            for copy in put(k, n):
-                copy.start()
+    def finish_piece(k, n):
+        part1(k, n, x).wait_recv()
+        rows = pl.ds(pl.multiple_of(rows_of(x, y, c, k) + n * (seq // CUTS), seq // CUTS), seq // CUTS)
+        out[rows, :] = (acc[k, cut(n), :] + out[rows, :].astype(F32)).astype(BF16)
+        for copy in put(k, n):
+            copy.start()
+
+    def finish(k, first=0):
+        for n in range(first, CUTS):
+            finish_piece(k, n)
         put_core(k).start()
 
     def pass_x(k, n):
@@ -453,9 +456,9 @@
             def _():
                 near(t + 1, slot // 2 + slot // 3)
 
-            @pl.when((t == 7) & (slot >= 2))
+            @pl.when((t == 7) & (slot % 2 == 1))
             def _():
-                pass_x(1, slot - 2)
+                finish_piece(2, slot // 2)
 
         @pl.when(jnp.logical_not(theirs))
         def _():
@@ -470,13 +473,10 @@
         def _():
             finish(k_their)
 
-        @pl.when(t == 2)
+        @pl.when(t == 4)
         def _():
             for n in range(CUTS):
                 near(OWN - 1, n)
-
-        @pl.when(t == 4)
-        def _():
             start_part1(2)
 
         @pl.when(t == 5)
@@ -485,11 +485,10 @@
 
         @pl.when(t == 6)
         def _():
+            pass_x_all(1)
             start_part1(3)
 
-    for n in range(2, PARTS):
-        pass_x(1, n)
-    finish(2)
+    finish(2, 2)
     finish(3)
 
     for copy in biases:

time: 307 us -> 305 us (level)
  no operation moved by 1% of the time
where the time goes in v6:
time: 305 us
  Pallas kernels  298 us (98%)
  local copies, waits for them, and re-layouts  7.54 us (2%)
    pallas_call x1, Pallas kernels, per_device(): pl.pallas_call(fused, out_shape=(pltpu.VMEM((n_images * seq, dim), BF16),...  298 us
    unnamed x1, local copies, waits for them, and re-layouts  7.54 us

profile of v6, /device:TPU:0, one launch (start us, length us, event | category | flops | bytes accessed | tf_op | source)
XLA Modules:
  0.0 305.2 jit_solution(18069556666109912318)
XLA Ops:
  0.0 297.6 %shard_map.127 = (bf16[8192,1280]{1,0:T(8,128)(2,1)S(1)}, bf16[3,480,1280]{2,1,0:T(8,128)(2,1)}, bf16[3,160,1280]{2,1,0:T(8,128)(2,1)}, bf16[3,1280,640]{2,1,0:T(8,128)(2,1)}, bf16[3,640,1280]{2,1,0:T(8,128)(2,1)}) custom-call(bf16[8192,1280]{1,0:T(8,128)(2,1)} %bitcast.6, bf16[2,160,1280]{2,1,0:T(8,128)(2,1)} %bitcast.7, bf16[2,160,1280]{2,1,0:T(8,128)(2,1)} %bitcast.8, ...), custom_call_target="tpu_custom_call" | custom-call | tf_op jit(solution)/shard_map/pallas_call | solution.py:549
  297.6 7.5 %copy.15 = bf16[32,256,1280]{2,1,0:T(8,128)(2,1)} copy(bf16[32,256,1280]{2,1,0:T(8,128)(2,1)S(1)} %bitcast.5) | data formatting | bytes 41943040

commit v7 on v6

--- a/solution.py
+++ b/solution.py
@@ -94,16 +94,16 @@
     vmem = (vq, vo, v1, v2)
     land = (gq, go, g1, g2)
 
-    def moves(src, dst, send, recv, dev):
-        return [remote(src[q], dst[q], send, recv.at[q], dev) for q in range(PIECES)]
+    def moves(src, dst, send, recv, dev, together=False):
+        return [remote(src[q], dst[q], send, recv if together else recv.at[q], dev) for q in range(PIECES)]
 
     own_load = [pltpu.make_async_copy(pieces_of(0)[q], slot_of(vmem, 0)[q], loc0) for q in range(PIECES)]
-    own_core = moves(pieces_of(0), slot_of(vmem, 1), s_c0, r_c0, cp)
+    own_core = moves(pieces_of(0), slot_of(vmem, 1), s_c0, r_c0, cp, True)
     own_x = moves(pieces_of(0), slot_of(vmem, 2), s_x0, r_x0, xp)
     fwd_x = moves(slot_of(vmem, 2), slot_of(vmem, 3), s_f0, r_f0, cp)
-    nxt_core = moves(pieces_of(1), slot_of(land, 0), s_c1, r_c1, cp)
+    nxt_core = moves(pieces_of(1), slot_of(land, 0), s_c1, r_c1, cp, True)
     nxt_y = moves(pieces_of(1), slot_of(land, 1), s_y1, r_y1, yp)
-    fwd_y = moves(slot_of(land, 1), slot_of(land, 2), s_f1, r_f1, cp)
+    fwd_y = moves(slot_of(land, 1), slot_of(land, 2), s_f1, r_f1, cp, True)
     peers = (cp, xp, xc, yp, yc)
     biases = [remote(bu, vb.at[n + 1], s_b.at[n], r_b.at[n], peers[n]) for n in range(5)]
 
@@ -136,11 +136,12 @@
         own_load[q].start()
     pl.semaphore_wait(barrier, len(peers))
 
-    for copy in biases:
-        copy.start()
     for q in range(PIECES):
         own_x[q].start()
         nxt_y[q].start()
+        if q == 3:
+            for copy in biases:
+                copy.start()
         own_core[q].start()
     for q in range(PIECES):
         nxt_core[q].start()
@@ -233,24 +234,24 @@
         @pl.when(slot == 0)
         def _():
             filled(loc0, BLOCK)
-            for copy in biases:
-                copy.wait_recv()
 
         @pl.when(slot == 1)
         def _():
-            for q in range(PIECES):
-                own_core[q].wait_recv()
+            biases[0].wait_recv()
+            filled(r_c0, BLOCK)
 
         @pl.loop(0, IMGS)
         def _(i):
             acc[i] += both(i, slot, 0)
 
-    for q in range(PIECES):
-        nxt_core[q].wait_recv()
+    filled(r_c1, BLOCK)
     for q in range(PIECES):
         nxt_load(0, q).start()
         nxt_load(1, q).start()
 
+    for copy in biases[1:]:
+        copy.wait_recv()
+
     def arrive(slot, pieces):
         @pl.when(slot == 2)
         def _():
@@ -290,6 +291,11 @@
     for q in (6, 7):
         own_x[q].wait_recv()
         fwd_x[q].start()
+
+    @pl.loop(0, 2)
+    def _(mine):
+        acc[OWN * mine] += mlp_part(OWN * mine, 2, 0, SPLIT, mlp)
+
     for q in (6, 7):
         fwd_x[q].wait_recv()
 
@@ -323,7 +329,14 @@
         @pl.loop(0, 2)
         def _(mine):
             i = k + OWN * mine
-            acc[i] += mlp_part(i, 2, 0, SPLIT, mlp) + mlp_part(i, 3, 0, SPLIT, mlp)
+
+            @pl.when(k == 0)
+            def _():
+                acc[i] += mlp_part(i, 3, 0, SPLIT, mlp)
+
+            @pl.when(k > 0)
+            def _():
+                acc[i] += mlp_part(i, 2, 0, SPLIT, mlp) + mlp_part(i, 3, 0, SPLIT, mlp)
 
             @pl.when(mine == 0)
             def _():
@@ -344,8 +357,7 @@
     sent(s_f0, BLOCK)
     for q in range(PIECES):
         nxt_load(2, q).start()
-    for q in range(PIECES):
-        fwd_y[q].wait_recv()
+    filled(r_f1, BLOCK)
     for q in range(PIECES):
         nxt_load(3, q).start()
 
@@ -570,7 +582,8 @@
                 pltpu.VMEM((OWN, seq, dim), BF16),
                 dma(6),
                 one, dma(4), dma(IMGS), dma(5), dma(5),
-                *[one, dma(PIECES)] * 6,
+                one, one, *[one, dma(PIECES)] * 2,
+                one, one, one, dma(PIECES), one, one,
                 *[dma(OWN), dma(OWN, CUTS)] * 2, one, dma(OWN, CUTS),
                 *[one] * 4,
                 *[one, dma(OWN, PARTS)] * 3,

time: 305 us -> 304 us (level)
  no operation moved by 1% of the time
where the time goes in v7:
time: 304 us
  Pallas kernels  297 us (98%)
  local copies, waits for them, and re-layouts  7.54 us (2%)
    pallas_call x1, Pallas kernels, per_device(): pl.pallas_call(fused, out_shape=(pltpu.VMEM((n_images * seq, dim), BF16),...  297 us
    unnamed x1, local copies, waits for them, and re-layouts  7.54 us

profile of v7, /device:TPU:0, one launch (start us, length us, event | category | flops | bytes accessed | tf_op | source)
XLA Modules:
  0.0 304.3 jit_solution(7157127955037325815)
XLA Ops:
  0.0 296.8 %shard_map.127 = (bf16[8192,1280]{1,0:T(8,128)(2,1)S(1)}, bf16[3,480,1280]{2,1,0:T(8,128)(2,1)}, bf16[3,160,1280]{2,1,0:T(8,128)(2,1)}, bf16[3,1280,640]{2,1,0:T(8,128)(2,1)}, bf16[3,640,1280]{2,1,0:T(8,128)(2,1)}) custom-call(bf16[8192,1280]{1,0:T(8,128)(2,1)} %bitcast.6, bf16[2,160,1280]{2,1,0:T(8,128)(2,1)} %bitcast.7, bf16[2,160,1280]{2,1,0:T(8,128)(2,1)} %bitcast.8, ...), custom_call_target="tpu_custom_call" | custom-call | tf_op jit(solution)/shard_map/pallas_call | solution.py:561
  296.8 7.5 %copy.15 = bf16[32,256,1280]{2,1,0:T(8,128)(2,1)} copy(bf16[32,256,1280]{2,1,0:T(8,128)(2,1)S(1)} %bitcast.5) | data formatting | bytes 41943040

commit v8 on v7

--- a/solution.py
+++ b/solution.py
@@ -292,9 +292,7 @@
         own_x[q].wait_recv()
         fwd_x[q].start()
 
-    @pl.loop(0, 2)
-    def _(mine):
-        acc[OWN * mine] += mlp_part(OWN * mine, 2, 0, SPLIT, mlp)
+    acc[0] += mlp_part(0, 2, 0, SPLIT, mlp)
 
     for q in (6, 7):
         fwd_x[q].wait_recv()
@@ -330,11 +328,11 @@
         def _(mine):
             i = k + OWN * mine
 
-            @pl.when(k == 0)
+            @pl.when(i == 0)
             def _():
                 acc[i] += mlp_part(i, 3, 0, SPLIT, mlp)
 
-            @pl.when(k > 0)
+            @pl.when(i > 0)
             def _():
                 acc[i] += mlp_part(i, 2, 0, SPLIT, mlp) + mlp_part(i, 3, 0, SPLIT, mlp)
 

time: 304 us -> 305 us (level)
  no operation moved by 1% of the time
where the time goes in v8:
time: 305 us
  Pallas kernels  297 us (97%)
  local copies, waits for them, and re-layouts  7.54 us (2%)
    pallas_call x1, Pallas kernels, per_device(): pl.pallas_call(fused, out_shape=(pltpu.VMEM((n_images * seq, dim), BF16),...  297 us
    unnamed x1, local copies, waits for them, and re-layouts  7.54 us

profile of v8, /device:TPU:0, one launch (start us, length us, event | category | flops | bytes accessed | tf_op | source)
XLA Modules:
  0.0 304.8 jit_solution(11563635798250626747)
XLA Ops:
  0.0 297.2 %shard_map.127 = (bf16[8192,1280]{1,0:T(8,128)(2,1)S(1)}, bf16[3,480,1280]{2,1,0:T(8,128)(2,1)}, bf16[3,160,1280]{2,1,0:T(8,128)(2,1)}, bf16[3,1280,640]{2,1,0:T(8,128)(2,1)}, bf16[3,640,1280]{2,1,0:T(8,128)(2,1)}) custom-call(bf16[8192,1280]{1,0:T(8,128)(2,1)} %bitcast.6, bf16[2,160,1280]{2,1,0:T(8,128)(2,1)} %bitcast.7, bf16[2,160,1280]{2,1,0:T(8,128)(2,1)} %bitcast.8, ...), custom_call_target="tpu_custom_call" | custom-call | tf_op jit(solution)/shard_map/pallas_call | solution.py:559
  297.2 7.5 %copy.15 = bf16[32,256,1280]{2,1,0:T(8,128)(2,1)} copy(bf16[32,256,1280]{2,1,0:T(8,128)(2,1)S(1)} %bitcast.5) | data formatting | bytes 41943040
